TPU v7x, 128 devices: a whole 4x4x4 slice. The times are simulated.
128 devices in a mesh: pipe: 4 (over y_hi, core), exp: 16 (over x, z), pair: 2 (over y_lo).
Axes of the slice: x: 4, y: 4 (y_hi: 2, y_lo: 2; y = y_hi * 2 + y_lo), z: 4, core: 2. Of those that a mesh axis runs over, the one named last changes fastest.
Arguments:
- hidden_in: bfloat16 [4, 1024, 2048], P(None, ('exp', 'pair')), may hold values from -6 to 6
- routes: int32 [4, 4, 1024, 8], P('pipe', None, ('exp', 'pair')), may hold values from 0 to 63, all different within a row; in each aligned block of 32 rows (0 to 31, 32 to 63, ..., all dimensions but the last counted through in order) at most 6 rows name the same one
- gate_probs: float32 [4, 4, 1024, 8], P('pipe', None, ('exp', 'pair')), may hold values from 0.02 to 1
- norm_gain: float32 [4, 2048], P('pipe'), may hold values from 0.1 to 1.9
- w_gate: bfloat16 [4, 64, 2048, 768], P('pipe', ('exp', 'pair')), may hold values from -0.125 to 0.125
- w_up: bfloat16 [4, 64, 2048, 768], P('pipe', ('exp', 'pair')), may hold values from -0.125 to 0.125
- w_down: bfloat16 [4, 64, 768, 2048], P('pipe', ('exp', 'pair')), may hold values from -0.21875 to 0.21875
Outputs:
- layer_outputs: bfloat16 [4, 4, 1024, 2048], P('pipe', None, ('exp', 'pair'))
Inputs may be any that keep to these rules, and one draw needn't show every extreme that they name: `routes`: within each layer and micro-batch, the 32 tokens of one device (aligned blocks) name no expert more than 6 times in all, and each token names 8 different experts.
All inputs are finite; a program needn't handle non-finite values.
Results may differ from a plain program's by a relative error of at most 0.01.
Values may be sent and summed in bfloat16 or wider, within the bound.
No kernel may reach another device: no remote copies, remote signals or barrier semaphores. Data moves between devices by JAX's collectives and lax.ppermute only.
A program may use at most 64 MiB of HBM per device.

v0:
```python
import jax
import jax.numpy as jnp
from jax import lax
from jax.sharding import PartitionSpec as P

EPS = 1e-06


def passed_along(value, axis, steps):
    count = lax.axis_size(axis)
    first, last = (max(0, -steps), min(count, count - steps))
    return lax.ppermute(value, axis, [(source, source + steps) for source in range(first, last)])


def expert_block(arrived, wgate, wupper, wdown):
    gate = jnp.einsum("nlcd,ldf->nlcf", arrived, wgate, preferred_element_type=jnp.float32)
    upward = jnp.einsum("nlcd,ldf->nlcf", arrived, wupper, preferred_element_type=jnp.float32)
    hidden = (jax.nn.silu(gate) * upward).astype(jnp.bfloat16)
    return jnp.einsum("nlcf,lfd->nlcd", hidden, wdown, preferred_element_type=jnp.float32).astype(
        jnp.bfloat16
    )


def on_device(hidden_in, routes, gate_probs, norm_gain, w_gate, w_up, w_down):
    section = lax.axis_index("pipe")
    micro, tok_rows, width = hidden_in.shape
    top_count = routes.shape[3]
    groups = lax.axis_size(("exp", "pair"))
    local_experts = w_gate.shape[1]
    experts = local_experts * groups
    capacity = max(2, 3 * tok_rows * top_count // (2 * experts))
    gain = norm_gain[0]
    wgate = w_gate[0]
    wupper = w_up[0]
    wdown = w_down[0]
    expert_ids = jnp.arange(experts, dtype=jnp.int32)

    def layer(state, index):
        chosen = lax.dynamic_index_in_dim(routes[0], index, 0, keepdims=False).reshape(-1)
        probs = lax.dynamic_index_in_dim(gate_probs[0], index, 0, keepdims=False)
        floated = state.astype(jnp.float32)
        scale = lax.rsqrt(jnp.mean(floated * floated, axis=-1, keepdims=True) + EPS)
        normed = (floated * scale * gain).astype(jnp.bfloat16)
        onehot = (chosen[:, None] == expert_ids[None, :]).astype(jnp.int32)
        before = jnp.cumsum(onehot, axis=0) - onehot
        slots = jnp.sum(before * onehot, axis=1)
        outgoing = jnp.zeros((experts, capacity, width), jnp.bfloat16)
        outgoing = outgoing.at[chosen, slots].set(jnp.repeat(normed, top_count, axis=0))
        grouped = outgoing.reshape(groups, local_experts, capacity, width)
        produced = expert_block(
            lax.all_to_all(grouped, ("exp", "pair"), split_axis=0, concat_axis=0, tiled=True),
            wgate,
            wupper,
            wdown,
        )
        returned = lax.all_to_all(
            produced, ("exp", "pair"), split_axis=0, concat_axis=0, tiled=True
        )
        results = returned.reshape(experts, capacity, width)[chosen, slots]
        results = results.reshape(tok_rows, top_count, width).astype(jnp.float32)
        weights = probs / jnp.sum(probs, axis=-1, keepdims=True)
        mixed = jnp.einsum("tk,tkd->td", weights, results)
        return (floated + mixed).astype(jnp.bfloat16)

    def advance(step, carry):
        received, saved = carry
        index = step - section
        valid = jnp.logical_and(index >= 0, index < micro)
        clipped = jnp.clip(index, 0, micro - 1)
        first = lax.dynamic_index_in_dim(hidden_in, clipped, 0, keepdims=False)
        state = jnp.where(section == 0, first, received)
        updated = layer(state, clipped)
        saved = jnp.where(valid, lax.dynamic_update_index_in_dim(saved, updated, clipped, 0), saved)
        received = passed_along(updated, "pipe", 1)
        return (received, saved)

    start = (
        jnp.zeros((tok_rows, width), jnp.bfloat16),
        jnp.zeros((micro, tok_rows, width), jnp.bfloat16),
    )
    received, saved = lax.fori_loop(0, micro + lax.axis_size("pipe") - 1, advance, start)
    return saved[None]


def solution(mesh):
    in_specs = (
        P(None, ("exp", "pair"), None),
        P("pipe", None, ("exp", "pair"), None),
        P("pipe", None, ("exp", "pair"), None),
        P("pipe", None),
        P("pipe", ("exp", "pair"), None, None),
        P("pipe", ("exp", "pair"), None, None),
        P("pipe", ("exp", "pair"), None, None),
    )
    out_specs = P("pipe", None, ("exp", "pair"), None)
    return jax.shard_map(
        on_device, mesh=mesh, in_specs=in_specs, out_specs=out_specs, check_vma=False
    )
```

profile of v0, /device:TPU:1, one launch (start us, length us, event | category | flops | bytes accessed | tf_op | source)
XLA Modules:
  0.0 810.9 jit_solution(4806493436090635416)
XLA Ops:
  0.9 810.0 %while.18 = (s32[]{:T(128)}, bf16[32,2048]{1,0:T(8,128)(2,1)S(1)}, bf16[4,32,2048]{2,1,0:T(8,128)(2,1)}, pred[]{:T(512)}, s32[]{:T(128)}, /*index=5*/bf16[4,32,2...) while((s32[]{:T(128)}, bf16[32,2048]{1,0:T(8,128)(2,1)S(1)}, ...), condition=%wide.region_7.8_spmd.clone.clone, body=%wide.region_0.7_spmd.clone.clone.sunk | while | flops 3630486016 | bytes 61134680 | solution.py:81
  5.1 22.3 %scatter_fusion = bf16[64,6,2048]{2,0,1:T(8,128)(2,1)S(1)} fusion(bf16[64,6,2048]{2,0,1:T(8,128)(2,1)S(1)} %broadcast.267, s32[256]{0:T(256)S(1)} %bitcast.139, bf16[256,2048]{1,0:T(8,128)(2,1)S(1)} %broadcast_bitcast_fusion.2), kind=kCustom, calls=%fused_computation.1.clone.clone.1 | custom fusion | bytes 3147776 | tf_op jit(solution)/shard_map/while/body/eval_jaxpr/scatter | solution.py:48
  30.2 31.7 %all_to_all.26 = bf16[32,2,6,2048]{3,1,2,0:T(2,128)(2,1)S(1)} all-to-all(bf16[32,2,6,2048]{3,1,2,0:T(2,128)(2,1)S(1)} %copy.58), channel_id=1, replica_groups=mesh['pipe'=4,'exp'=16,'pair'=2] {'exp','pair'}, dimensions={0} | all-to-all | bytes 3145728 | tf_op jit(solution)/shard_map/while/body/eval_jaxpr/all_to_all | solution.py:51
  61.8 6.4 fusion.86
  68.2 8.9 %fusion.87 = bf16[32,2,6,2048]{3,0,2,1:T(8,128)(2,1)S(1)} fusion(bf16[2,768,2048]{2,1,0:T(8,128)(2,1)} %get-tuple-element.525, bf16[2,2048,768]{2,1,0:T(8,128)(2,1)} %get-tuple-element.524, bf16[32,2,6,2048]{3,1,2,0:T(2,128)(2,1)S(1)} %all_to_all.26, f32[32,2,6,768]{3,0,2,1:T(8,128)} %fusion.86), kind=kOutput, calls=%fused_computation.10.clone.1 | convolution fusion | flops 2418475008 | bytes 16908288 | tf_op jit(solution)/shard_map/while/body/eval_jaxpr/nlcf,lfd->nlcd/dot_general | solution.py:19
  79.9 4.5 all-to-all-start.1
  84.6 20.8 %all-to-all-done.1 = bf16[32,2,6,2048]{3,1,2,0:T(2,128)(2,1)S(1)} async-done(((bf16[32,2,6,2048]{3,1,2,0:T(2,128)(2,1)}), bf16[32,2,6,2048]{3,1,2,0:T(2,128)(2,1)S(1)}, u32[]{:S(2)}, u32[]{:S(2)}) %all-to-all-start.1) | async-done | bytes 1572896 | tf_op jit(solution)/shard_map/while/body/eval_jaxpr/all_to_all | solution.py:56
  107.2 4.3 gather_fusion
  113.6 7.3 collective-permute-start
  127.1 22.3 %scatter_fusion = bf16[64,6,2048]{2,0,1:T(8,128)(2,1)S(1)} fusion(bf16[64,6,2048]{2,0,1:T(8,128)(2,1)S(1)} %broadcast.267, s32[256]{0:T(256)S(1)} %bitcast.139, bf16[256,2048]{1,0:T(8,128)(2,1)S(1)} %broadcast_bitcast_fusion.2), kind=kCustom, calls=%fused_computation.1.clone.clone.1 | custom fusion | bytes 3147776 | tf_op jit(solution)/shard_map/while/body/eval_jaxpr/scatter | solution.py:48
  152.1 25.0 %all_to_all.26 = bf16[32,2,6,2048]{3,1,2,0:T(2,128)(2,1)S(1)} all-to-all(bf16[32,2,6,2048]{3,1,2,0:T(2,128)(2,1)S(1)} %copy.58), channel_id=1, replica_groups=mesh['pipe'=4,'exp'=16,'pair'=2] {'exp','pair'}, dimensions={0} | all-to-all | bytes 3145728 | tf_op jit(solution)/shard_map/while/body/eval_jaxpr/all_to_all | solution.py:51
  177.1 6.4 fusion.86
  183.6 8.9 %fusion.87 = bf16[32,2,6,2048]{3,0,2,1:T(8,128)(2,1)S(1)} fusion(bf16[2,768,2048]{2,1,0:T(8,128)(2,1)} %get-tuple-element.525, bf16[2,2048,768]{2,1,0:T(8,128)(2,1)} %get-tuple-element.524, bf16[32,2,6,2048]{3,1,2,0:T(2,128)(2,1)S(1)} %all_to_all.26, f32[32,2,6,768]{3,0,2,1:T(8,128)} %fusion.86), kind=kOutput, calls=%fused_computation.10.clone.1 | convolution fusion | flops 2418475008 | bytes 16908288 | tf_op jit(solution)/shard_map/while/body/eval_jaxpr/nlcf,lfd->nlcd/dot_general | solution.py:19
  199.5 22.2 %all-to-all-done.1 = bf16[32,2,6,2048]{3,1,2,0:T(2,128)(2,1)S(1)} async-done(((bf16[32,2,6,2048]{3,1,2,0:T(2,128)(2,1)}), bf16[32,2,6,2048]{3,1,2,0:T(2,128)(2,1)S(1)}, u32[]{:S(2)}, u32[]{:S(2)}) %all-to-all-start.1) | async-done | bytes 1572896 | tf_op jit(solution)/shard_map/while/body/eval_jaxpr/all_to_all | solution.py:56
  223.6 4.3 gather_fusion
  238.1 22.3 %scatter_fusion = bf16[64,6,2048]{2,0,1:T(8,128)(2,1)S(1)} fusion(bf16[64,6,2048]{2,0,1:T(8,128)(2,1)S(1)} %broadcast.267, s32[256]{0:T(256)S(1)} %bitcast.139, bf16[256,2048]{1,0:T(8,128)(2,1)S(1)} %broadcast_bitcast_fusion.2), kind=kCustom, calls=%fused_computation.1.clone.clone.1 | custom fusion | bytes 3147776 | tf_op jit(solution)/shard_map/while/body/eval_jaxpr/scatter | solution.py:48
  263.1 28.4 %all_to_all.26 = bf16[32,2,6,2048]{3,1,2,0:T(2,128)(2,1)S(1)} all-to-all(bf16[32,2,6,2048]{3,1,2,0:T(2,128)(2,1)S(1)} %copy.58), channel_id=1, replica_groups=mesh['pipe'=4,'exp'=16,'pair'=2] {'exp','pair'}, dimensions={0} | all-to-all | bytes 3145728 | tf_op jit(solution)/shard_map/while/body/eval_jaxpr/all_to_all | solution.py:51
  291.5 6.4 fusion.86
  297.9 8.9 %fusion.87 = bf16[32,2,6,2048]{3,0,2,1:T(8,128)(2,1)S(1)} fusion(bf16[2,768,2048]{2,1,0:T(8,128)(2,1)} %get-tuple-element.525, bf16[2,2048,768]{2,1,0:T(8,128)(2,1)} %get-tuple-element.524, bf16[32,2,6,2048]{3,1,2,0:T(2,128)(2,1)S(1)} %all_to_all.26, f32[32,2,6,768]{3,0,2,1:T(8,128)} %fusion.86), kind=kOutput, calls=%fused_computation.10.clone.1 | convolution fusion | flops 2418475008 | bytes 16908288 | tf_op jit(solution)/shard_map/while/body/eval_jaxpr/nlcf,lfd->nlcd/dot_general | solution.py:19
  309.6 4.7 all-to-all-start.1
  314.5 22.2 %all-to-all-done.1 = bf16[32,2,6,2048]{3,1,2,0:T(2,128)(2,1)S(1)} async-done(((bf16[32,2,6,2048]{3,1,2,0:T(2,128)(2,1)}), bf16[32,2,6,2048]{3,1,2,0:T(2,128)(2,1)S(1)}, u32[]{:S(2)}, u32[]{:S(2)}) %all-to-all-start.1) | async-done | bytes 1572896 | tf_op jit(solution)/shard_map/while/body/eval_jaxpr/all_to_all | solution.py:56
  338.6 4.3 gather_fusion
  353.1 22.3 %scatter_fusion = bf16[64,6,2048]{2,0,1:T(8,128)(2,1)S(1)} fusion(bf16[64,6,2048]{2,0,1:T(8,128)(2,1)S(1)} %broadcast.267, s32[256]{0:T(256)S(1)} %bitcast.139, bf16[256,2048]{1,0:T(8,128)(2,1)S(1)} %broadcast_bitcast_fusion.2), kind=kCustom, calls=%fused_computation.1.clone.clone.1 | custom fusion | bytes 3147776 | tf_op jit(solution)/shard_map/while/body/eval_jaxpr/scatter | solution.py:48
  378.1 28.9 %all_to_all.26 = bf16[32,2,6,2048]{3,1,2,0:T(2,128)(2,1)S(1)} all-to-all(bf16[32,2,6,2048]{3,1,2,0:T(2,128)(2,1)S(1)} %copy.58), channel_id=1, replica_groups=mesh['pipe'=4,'exp'=16,'pair'=2] {'exp','pair'}, dimensions={0} | all-to-all | bytes 3145728 | tf_op jit(solution)/shard_map/while/body/eval_jaxpr/all_to_all | solution.py:51
  407.0 6.4 fusion.86
  413.4 8.9 %fusion.87 = bf16[32,2,6,2048]{3,0,2,1:T(8,128)(2,1)S(1)} fusion(bf16[2,768,2048]{2,1,0:T(8,128)(2,1)} %get-tuple-element.525, bf16[2,2048,768]{2,1,0:T(8,128)(2,1)} %get-tuple-element.524, bf16[32,2,6,2048]{3,1,2,0:T(2,128)(2,1)S(1)} %all_to_all.26, f32[32,2,6,768]{3,0,2,1:T(8,128)} %fusion.86), kind=kOutput, calls=%fused_computation.10.clone.1 | convolution fusion | flops 2418475008 | bytes 16908288 | tf_op jit(solution)/shard_map/while/body/eval_jaxpr/nlcf,lfd->nlcd/dot_general | solution.py:19
  425.1 4.8 all-to-all-start.1
  430.0 22.2 %all-to-all-done.1 = bf16[32,2,6,2048]{3,1,2,0:T(2,128)(2,1)S(1)} async-done(((bf16[32,2,6,2048]{3,1,2,0:T(2,128)(2,1)}), bf16[32,2,6,2048]{3,1,2,0:T(2,128)(2,1)S(1)}, u32[]{:S(2)}, u32[]{:S(2)}) %all-to-all-start.1) | async-done | bytes 1572896 | tf_op jit(solution)/shard_map/while/body/eval_jaxpr/all_to_all | solution.py:56
  454.1 4.3 gather_fusion
  468.6 22.3 %scatter_fusion = bf16[64,6,2048]{2,0,1:T(8,128)(2,1)S(1)} fusion(bf16[64,6,2048]{2,0,1:T(8,128)(2,1)S(1)} %broadcast.267, s32[256]{0:T(256)S(1)} %bitcast.139, bf16[256,2048]{1,0:T(8,128)(2,1)S(1)} %broadcast_bitcast_fusion.2), kind=kCustom, calls=%fused_computation.1.clone.clone.1 | custom fusion | bytes 3147776 | tf_op jit(solution)/shard_map/while/body/eval_jaxpr/scatter | solution.py:48
  493.6 28.8 %all_to_all.26 = bf16[32,2,6,2048]{3,1,2,0:T(2,128)(2,1)S(1)} all-to-all(bf16[32,2,6,2048]{3,1,2,0:T(2,128)(2,1)S(1)} %copy.58), channel_id=1, replica_groups=mesh['pipe'=4,'exp'=16,'pair'=2] {'exp','pair'}, dimensions={0} | all-to-all | bytes 3145728 | tf_op jit(solution)/shard_map/while/body/eval_jaxpr/all_to_all | solution.py:51
  522.4 6.4 fusion.86
  528.9 8.9 %fusion.87 = bf16[32,2,6,2048]{3,0,2,1:T(8,128)(2,1)S(1)} fusion(bf16[2,768,2048]{2,1,0:T(8,128)(2,1)} %get-tuple-element.525, bf16[2,2048,768]{2,1,0:T(8,128)(2,1)} %get-tuple-element.524, bf16[32,2,6,2048]{3,1,2,0:T(2,128)(2,1)S(1)} %all_to_all.26, f32[32,2,6,768]{3,0,2,1:T(8,128)} %fusion.86), kind=kOutput, calls=%fused_computation.10.clone.1 | convolution fusion | flops 2418475008 | bytes 16908288 | tf_op jit(solution)/shard_map/while/body/eval_jaxpr/nlcf,lfd->nlcd/dot_general | solution.py:19
  540.6 4.8 all-to-all-start.1
  545.5 22.2 %all-to-all-done.1 = bf16[32,2,6,2048]{3,1,2,0:T(2,128)(2,1)S(1)} async-done(((bf16[32,2,6,2048]{3,1,2,0:T(2,128)(2,1)}), bf16[32,2,6,2048]{3,1,2,0:T(2,128)(2,1)S(1)}, u32[]{:S(2)}, u32[]{:S(2)}) %all-to-all-start.1) | async-done | bytes 1572896 | tf_op jit(solution)/shard_map/while/body/eval_jaxpr/all_to_all | solution.py:56
  584.1 22.3 %scatter_fusion = bf16[64,6,2048]{2,0,1:T(8,128)(2,1)S(1)} fusion(bf16[64,6,2048]{2,0,1:T(8,128)(2,1)S(1)} %broadcast.267, s32[256]{0:T(256)S(1)} %bitcast.139, bf16[256,2048]{1,0:T(8,128)(2,1)S(1)} %broadcast_bitcast_fusion.2), kind=kCustom, calls=%fused_computation.1.clone.clone.1 | custom fusion | bytes 3147776 | tf_op jit(solution)/shard_map/while/body/eval_jaxpr/scatter | solution.py:48
  609.1 28.9 %all_to_all.26 = bf16[32,2,6,2048]{3,1,2,0:T(2,128)(2,1)S(1)} all-to-all(bf16[32,2,6,2048]{3,1,2,0:T(2,128)(2,1)S(1)} %copy.58), channel_id=1, replica_groups=mesh['pipe'=4,'exp'=16,'pair'=2] {'exp','pair'}, dimensions={0} | all-to-all | bytes 3145728 | tf_op jit(solution)/shard_map/while/body/eval_jaxpr/all_to_all | solution.py:51
  638.0 6.4 fusion.86
  644.4 8.9 %fusion.87 = bf16[32,2,6,2048]{3,0,2,1:T(8,128)(2,1)S(1)} fusion(bf16[2,768,2048]{2,1,0:T(8,128)(2,1)} %get-tuple-element.525, bf16[2,2048,768]{2,1,0:T(8,128)(2,1)} %get-tuple-element.524, bf16[32,2,6,2048]{3,1,2,0:T(2,128)(2,1)S(1)} %all_to_all.26, f32[32,2,6,768]{3,0,2,1:T(8,128)} %fusion.86), kind=kOutput, calls=%fused_computation.10.clone.1 | convolution fusion | flops 2418475008 | bytes 16908288 | tf_op jit(solution)/shard_map/while/body/eval_jaxpr/nlcf,lfd->nlcd/dot_general | solution.py:19
  656.1 4.8 all-to-all-start.1
  661.0 22.2 %all-to-all-done.1 = bf16[32,2,6,2048]{3,1,2,0:T(2,128)(2,1)S(1)} async-done(((bf16[32,2,6,2048]{3,1,2,0:T(2,128)(2,1)}), bf16[32,2,6,2048]{3,1,2,0:T(2,128)(2,1)S(1)}, u32[]{:S(2)}, u32[]{:S(2)}) %all-to-all-start.1) | async-done | bytes 1572896 | tf_op jit(solution)/shard_map/while/body/eval_jaxpr/all_to_all | solution.py:56
  685.1 4.3 gather_fusion
  699.6 22.3 %scatter_fusion = bf16[64,6,2048]{2,0,1:T(8,128)(2,1)S(1)} fusion(bf16[64,6,2048]{2,0,1:T(8,128)(2,1)S(1)} %broadcast.267, s32[256]{0:T(256)S(1)} %bitcast.139, bf16[256,2048]{1,0:T(8,128)(2,1)S(1)} %broadcast_bitcast_fusion.2), kind=kCustom, calls=%fused_computation.1.clone.clone.1 | custom fusion | bytes 3147776 | tf_op jit(solution)/shard_map/while/body/eval_jaxpr/scatter | solution.py:48
  724.6 28.9 %all_to_all.26 = bf16[32,2,6,2048]{3,1,2,0:T(2,128)(2,1)S(1)} all-to-all(bf16[32,2,6,2048]{3,1,2,0:T(2,128)(2,1)S(1)} %copy.58), channel_id=1, replica_groups=mesh['pipe'=4,'exp'=16,'pair'=2] {'exp','pair'}, dimensions={0} | all-to-all | bytes 3145728 | tf_op jit(solution)/shard_map/while/body/eval_jaxpr/all_to_all | solution.py:51
  753.5 6.4 fusion.86
  760.0 8.9 %fusion.87 = bf16[32,2,6,2048]{3,0,2,1:T(8,128)(2,1)S(1)} fusion(bf16[2,768,2048]{2,1,0:T(8,128)(2,1)} %get-tuple-element.525, bf16[2,2048,768]{2,1,0:T(8,128)(2,1)} %get-tuple-element.524, bf16[32,2,6,2048]{3,1,2,0:T(2,128)(2,1)S(1)} %all_to_all.26, f32[32,2,6,768]{3,0,2,1:T(8,128)} %fusion.86), kind=kOutput, calls=%fused_computation.10.clone.1 | convolution fusion | flops 2418475008 | bytes 16908288 | tf_op jit(solution)/shard_map/while/body/eval_jaxpr/nlcf,lfd->nlcd/dot_general | solution.py:19
  771.6 4.8 all-to-all-start.1
  776.6 22.2 %all-to-all-done.1 = bf16[32,2,6,2048]{3,1,2,0:T(2,128)(2,1)S(1)} async-done(((bf16[32,2,6,2048]{3,1,2,0:T(2,128)(2,1)}), bf16[32,2,6,2048]{3,1,2,0:T(2,128)(2,1)S(1)}, u32[]{:S(2)}, u32[]{:S(2)}) %all-to-all-start.1) | async-done | bytes 1572896 | tf_op jit(solution)/shard_map/while/body/eval_jaxpr/all_to_all | solution.py:56
  (221 shorter events, 134.3 us)
Async XLA Ops:
  79.9 4.5 copy-start
  79.9 25.5 %all-to-all-start.1 = ((bf16[32,2,6,2048]{3,1,2,0:T(2,128)(2,1)}), bf16[32,2,6,2048]{3,1,2,0:T(2,128)(2,1)S(1)}, u32[]{:S(2)}, u32[]{:S(2)}) async-start(bf16[32,2,6,2048]{3,1,2,0:T(2,128)(2,1)} %copy.59), calls=%async_computation.1 | async-start | bytes 3145728 | tf_op jit(solution)/shard_map/while/body/eval_jaxpr/all_to_all | solution.py:56
  113.6 9.2 %collective-permute-start = (bf16[32,2048]{1,0:T(8,128)(2,1)S(1)}, bf16[32,2048]{1,0:T(8,128)(2,1)S(1)}, u32[]{:S(2)}, u32[]{:S(2)}) collective-permute-start(bf16[32,2048]{1,0:T(8,128)(2,1)S(1)} %get-tuple-element.478), channel_id=1, source_target_pairs={{0,32},{32,64},{64,96},{1,33},{33,65},{65,97},{2,34},{34,66},{66,9... | collective-permute-start | bytes 393224 | tf_op jit(solution)/shard_map/while/body/eval_jaxpr/ppermute | solution.py:12
  195.2 4.1 copy-start
  195.3 26.5 %all-to-all-start.1 = ((bf16[32,2,6,2048]{3,1,2,0:T(2,128)(2,1)}), bf16[32,2,6,2048]{3,1,2,0:T(2,128)(2,1)S(1)}, u32[]{:S(2)}, u32[]{:S(2)}) async-start(bf16[32,2,6,2048]{3,1,2,0:T(2,128)(2,1)} %copy.59), calls=%async_computation.1 | async-start | bytes 3145728 | tf_op jit(solution)/shard_map/while/body/eval_jaxpr/all_to_all | solution.py:56
  230.0 3.8 collective-permute-start
  309.6 4.8 copy-start
  309.6 27.2 %all-to-all-start.1 = ((bf16[32,2,6,2048]{3,1,2,0:T(2,128)(2,1)}), bf16[32,2,6,2048]{3,1,2,0:T(2,128)(2,1)S(1)}, u32[]{:S(2)}, u32[]{:S(2)}) async-start(bf16[32,2,6,2048]{3,1,2,0:T(2,128)(2,1)} %copy.59), calls=%async_computation.1 | async-start | bytes 3145728 | tf_op jit(solution)/shard_map/while/body/eval_jaxpr/all_to_all | solution.py:56
  345.0 3.8 collective-permute-start
  425.1 4.8 copy-start
  425.1 27.2 %all-to-all-start.1 = ((bf16[32,2,6,2048]{3,1,2,0:T(2,128)(2,1)}), bf16[32,2,6,2048]{3,1,2,0:T(2,128)(2,1)S(1)}, u32[]{:S(2)}, u32[]{:S(2)}) async-start(bf16[32,2,6,2048]{3,1,2,0:T(2,128)(2,1)} %copy.59), calls=%async_computation.1 | async-start | bytes 3145728 | tf_op jit(solution)/shard_map/while/body/eval_jaxpr/all_to_all | solution.py:56
  460.5 3.8 collective-permute-start
  540.5 4.8 copy-start
  540.6 27.2 %all-to-all-start.1 = ((bf16[32,2,6,2048]{3,1,2,0:T(2,128)(2,1)}), bf16[32,2,6,2048]{3,1,2,0:T(2,128)(2,1)S(1)}, u32[]{:S(2)}, u32[]{:S(2)}) async-start(bf16[32,2,6,2048]{3,1,2,0:T(2,128)(2,1)} %copy.59), calls=%async_computation.1 | async-start | bytes 3145728 | tf_op jit(solution)/shard_map/while/body/eval_jaxpr/all_to_all | solution.py:56
  576.0 3.8 collective-permute-start
  656.1 4.8 copy-start
  656.1 27.2 %all-to-all-start.1 = ((bf16[32,2,6,2048]{3,1,2,0:T(2,128)(2,1)}), bf16[32,2,6,2048]{3,1,2,0:T(2,128)(2,1)S(1)}, u32[]{:S(2)}, u32[]{:S(2)}) async-start(bf16[32,2,6,2048]{3,1,2,0:T(2,128)(2,1)} %copy.59), calls=%async_computation.1 | async-start | bytes 3145728 | tf_op jit(solution)/shard_map/while/body/eval_jaxpr/all_to_all | solution.py:56
  691.5 3.8 collective-permute-start
  771.6 4.8 copy-start
  771.6 27.2 %all-to-all-start.1 = ((bf16[32,2,6,2048]{3,1,2,0:T(2,128)(2,1)}), bf16[32,2,6,2048]{3,1,2,0:T(2,128)(2,1)S(1)}, u32[]{:S(2)}, u32[]{:S(2)}) async-start(bf16[32,2,6,2048]{3,1,2,0:T(2,128)(2,1)} %copy.59), calls=%async_computation.1 | async-start | bytes 3145728 | tf_op jit(solution)/shard_map/while/body/eval_jaxpr/all_to_all | solution.py:56
  807.1 3.8 collective-permute-start
where the time goes:
time: 813 us; the launch traced here: 811 us
  local copies, waits for them, and re-layouts  250 us (31%)
  blocking collectives  201 us (25%)
  waiting for transfers between devices  168 us (21%)
  matrix products  110 us (14%)
  starting transfers between devices  51.2 us (6%)
  other arithmetic  30.6 us (4%)
    all_to_all x7, blocking collectives, layer(): lax.all_to_all(grouped, ('exp', 'pair'), split_axis=0, concat_axis=0, til...  201 us
    scatter x7, local copies, waits for them, and re-layouts, layer(): outgoing.at[chosen, slots].set(jnp.repeat(normed, top_count, axis=0))  156 us
    all_to_all x7, waiting for transfers between devices, layer(): lax.all_to_all(produced, ('exp', 'pair'), split_axis=0, concat_axis=0, ti...  154 us
    dot_general x7, matrix products, expert_block(): jnp.einsum('nlcf,lfd->nlcd', hidden, wdown, preferred_element_type=jnp.fl...  62.3 us
    dot_general x7, matrix products, expert_block(): jnp.einsum('nlcd,ldf->nlcf', arrived, wgate, preferred_element_type=jnp.f...  45 us
    all_to_all x7, starting transfers between devices, layer(): lax.all_to_all(produced, ('exp', 'pair'), split_axis=0, concat_axis=0, ti...  32.4 us
    gather x7, local copies, waits for them, and re-layouts, layer(): results = returned.reshape(experts, capacity, width)[chosen, slots]  30.1 us
    convert_element_type x7, local copies, waits for them, and re-layouts, expert_block(): jnp.einsum('nlcf,lfd->nlcd', hidden, wdown, preferred_element_type=jnp.fl...  19.5 us
  transfers between devices with their start and end apart: 14, of which 14 were waited for; matrix products, arithmetic and copies ran while one was open for 0% of the time, Pallas kernels for 0%

commit v1 on v0

v1 whole, which is shorter than its diff:
```python
import functools

import jax
import jax.numpy as jnp
from jax import lax
from jax.experimental import pallas as pl
from jax.experimental.pallas import tpu as pltpu
from jax.sharding import PartitionSpec as P

EPS = 1e-06
F32 = jnp.float32
BF16 = jnp.bfloat16
GROUP = ("exp", "pair")


def dot(a, b):
    return jnp.dot(a, b, preferred_element_type=F32)


def dot_nt(a, b):
    return lax.dot_general(a, b, (((1,), (1,)), ((), ())), preferred_element_type=F32)


def iota(shape, dim):
    return lax.broadcasted_iota(jnp.int32, shape, dim)


def select_matrix(shape, source):
    return jnp.where(iota(shape, 1) == source(iota(shape, 0)), 1.0, 0.0).astype(BF16)


def naming(chosen, experts, values=None):
    tokens, top = chosen.shape
    ids = iota((tokens, experts), 1)
    total = jnp.zeros((tokens, experts), F32)
    for k in range(top):
        value = 1.0 if values is None else values[:, k : k + 1]
        total = total + jnp.where(chosen[:, k : k + 1] == ids, value, 0.0)
    return total


def rank_of(named):
    tokens = named.shape[0]
    earlier = jnp.where(iota((tokens, tokens), 1) < iota((tokens, tokens), 0), 1.0, 0.0)
    return dot(earlier.astype(BF16), named.astype(BF16))


def dispatch_kernel(where_ref, hidden_ref, received_ref, routes_ref, gain_ref, out_ref, state_ref):
    index = where_ref[0]
    experts = out_ref.shape[0] // 4
    width = hidden_ref.shape[2]
    half = width // 2
    state = jnp.where(where_ref[1] == 0, hidden_ref[index], received_ref[...])
    state_ref[...] = state
    floated = state.astype(F32)
    scale = lax.rsqrt(jnp.mean(floated * floated, axis=-1, keepdims=True) + EPS)
    normed = (floated * scale * gain_ref[...]).astype(BF16)
    named = naming(routes_ref[index], experts)
    rank = rank_of(named)
    spread = select_matrix((4 * experts, experts), lambda i: i >> 2)
    named_rows = dot_nt(spread, named.astype(BF16))
    rank_rows = dot_nt(spread, rank.astype(BF16)).astype(jnp.int32)
    row = iota(rank_rows.shape, 0)
    whole = jnp.where(rank_rows == (row & 3), named_rows, 0.0).astype(BF16)
    rest = jnp.where(rank_rows == 4 + ((row & 3) >> 1), named_rows, 0.0)
    left = jnp.where((row & 1) == 0, rest, 0.0).astype(BF16)
    right = jnp.where((row & 1) == 1, rest, 0.0).astype(BF16)
    out_ref[:, :width] = dot(whole, normed).astype(BF16)
    out_ref[:, width:] = (dot(left, normed[:, :half]) + dot(right, normed[:, half:])).astype(BF16)


def combine_kernel(where_ref, returned_ref, state_ref, routes_ref, probs_ref, updated_ref):
    index = where_ref[0]
    experts = returned_ref.shape[0] // 4
    tokens, width = state_ref.shape
    half = width // 2
    chosen = routes_ref[index]
    probs = probs_ref[index]
    weights = probs / jnp.sum(probs, axis=-1, keepdims=True)
    rank = rank_of(naming(chosen, experts))
    weight = naming(chosen, experts, weights)
    high = weight.astype(BF16)
    low = (weight - high.astype(F32)).astype(BF16)
    spread = select_matrix((4 * experts, experts), lambda i: i >> 2)
    rank_x = dot_nt(rank.astype(BF16), spread).astype(jnp.int32)
    both = jnp.concatenate([dot_nt(high, spread), dot_nt(low, spread)], axis=0)
    rank_x = jnp.concatenate([rank_x, rank_x], axis=0)
    col = iota(rank_x.shape, 1)
    whole = jnp.where(rank_x == (col & 3), both, 0.0).astype(BF16)
    rest = jnp.where(rank_x == 4 + ((col & 3) >> 1), both, 0.0)
    left = jnp.where((col & 1) == 0, rest, 0.0).astype(BF16)
    right = jnp.where((col & 1) == 1, rest, 0.0).astype(BF16)
    first = dot(whole, returned_ref[:, :width])
    tail = dot(jnp.concatenate([left, right], axis=0), returned_ref[:, width:])
    mixed = first[:tokens] + first[tokens:]
    mixed_left = tail[:tokens] + tail[tokens : 2 * tokens]
    mixed_right = tail[2 * tokens : 3 * tokens] + tail[3 * tokens :]
    floated = state_ref[...].astype(F32)
    updated_ref[:, :half] = (floated[:, :half] + mixed[:, :half] + mixed_left).astype(BF16)
    updated_ref[:, half:] = (floated[:, half:] + mixed[:, half:] + mixed_right).astype(BF16)


def expert_kernel(
    arrived_ref, gate_hbm, up_hbm, down_hbm, out_ref, gate_v, up_v, down_v, rows_v, acc_v, made_v, sems, *, cuts
):
    local, width, hidden = gate_v.shape
    groups = arrived_ref.shape[0] // 8
    half = width // 2
    cut = hidden // cuts

    def copies(e, f):
        part = pl.ds(f * cut, cut)
        return (
            pltpu.make_async_copy(gate_hbm.at[e, :, part], gate_v.at[e, :, part], sems.at[0, e, f]),
            pltpu.make_async_copy(up_hbm.at[e, :, part], up_v.at[e, :, part], sems.at[1, e, f]),
            pltpu.make_async_copy(down_hbm.at[e, part, :], down_v.at[e, part, :], sems.at[2, e, f]),
        )

    for e in range(local):
        for f in range(cuts):
            for copy in copies(e, f):
                copy.start()
    for e in range(local):
        pick = select_matrix((4 * groups, 8 * groups), lambda i: 8 * (i >> 2) + 4 * e + (i & 3))
        rows_v[: 4 * groups] = dot(pick, arrived_ref[:, :width]).astype(BF16)
        for q in range(2):
            pick = select_matrix((2 * groups, 8 * groups), lambda i: 8 * (i >> 1) + 4 * e + 2 * (i & 1) + q)
            rows_v[4 * groups :, q * half : (q + 1) * half] = dot(pick, arrived_ref[:, width:]).astype(BF16)
        for f in range(cuts):
            gate_copy, up_copy, down_copy = copies(e, f)
            part = slice(f * cut, (f + 1) * cut)
            gate_copy.wait()
            gate = dot(rows_v[...], gate_v[e, :, part])
            up_copy.wait()
            upward = dot(rows_v[...], up_v[e, :, part])
            mid = (jax.nn.silu(gate) * upward).astype(BF16)
            down_copy.wait()
            product = dot(mid, down_v[e, part, :])
            if f == 0:
                acc_v[...] = product
            elif f < cuts - 1:
                acc_v[...] += product
            else:
                made_v[e] = (acc_v[...] + product).astype(BF16)
    out = jnp.zeros((8 * groups, width), F32)
    tail = jnp.zeros((8 * groups, half), F32)
    for e in range(local):
        target = iota((8 * groups, 4 * groups), 0)
        place = jnp.where(
            (iota(target.shape, 1) == 4 * (target >> 3) + (target & 3)) & (((target >> 2) & 1) == e), 1.0, 0.0
        ).astype(BF16)
        out = out + dot(place, made_v[e, : 4 * groups])
        for q in range(2):
            target = iota((8 * groups, 2 * groups), 0)
            place = jnp.where(
                (iota(target.shape, 1) == 2 * (target >> 3) + ((target >> 1) & 1))
                & (((target >> 2) & 1) == e)
                & ((target & 1) == q),
                1.0,
                0.0,
            ).astype(BF16)
            tail = tail + dot(place, made_v[e, 4 * groups :, q * half : (q + 1) * half])
    out_ref[:, :width] = out.astype(BF16)
    out_ref[:, width:] = tail.astype(BF16)


def on_device(hidden_in, routes, gate_probs, norm_gain, w_gate, w_up, w_down):
    section = lax.axis_index("pipe")
    stages = lax.axis_size("pipe")
    micro, tokens, width = hidden_in.shape
    groups = lax.axis_size(GROUP)
    local, hidden = w_gate.shape[1], w_gate.shape[3]
    assert local == 2 and routes.shape[3] * tokens == 4 * local * groups
    rows = 8 * groups
    wide = width + width // 2
    smem = pl.BlockSpec(memory_space=pltpu.SMEM)
    vmem = pl.BlockSpec(memory_space=pltpu.VMEM)
    hbm = pl.BlockSpec(memory_space=pl.ANY)
    packet = jax.ShapeDtypeStruct((rows, wide), BF16)
    token_rows = jax.ShapeDtypeStruct((tokens, width), BF16)
    cuts = 3

    dispatch = pl.pallas_call(
        dispatch_kernel,
        out_shape=(packet, token_rows),
        in_specs=[smem, vmem, vmem, vmem, vmem],
        out_specs=(vmem, vmem),
        name="dispatch",
    )
    experts = pl.pallas_call(
        functools.partial(expert_kernel, cuts=cuts),
        out_shape=packet,
        in_specs=[vmem, hbm, hbm, hbm],
        out_specs=vmem,
        scratch_shapes=[
            pltpu.VMEM((local, width, hidden), BF16),
            pltpu.VMEM((local, width, hidden), BF16),
            pltpu.VMEM((local, hidden, width), BF16),
            pltpu.VMEM((6 * groups, width), BF16),
            pltpu.VMEM((6 * groups, width), F32),
            pltpu.VMEM((local, 6 * groups, width), BF16),
            pltpu.SemaphoreType.DMA((3, local, cuts)),
        ],
        compiler_params=pltpu.CompilerParams(vmem_limit_bytes=44 * 2**20),
        name="experts",
    )
    combine = pl.pallas_call(
        combine_kernel,
        out_shape=token_rows,
        in_specs=[smem, vmem, vmem, vmem, vmem],
        out_specs=vmem,
        name="combine",
    )

    def exchange(packets):
        return lax.all_to_all(packets, GROUP, split_axis=0, concat_axis=0, tiled=True)

    def advance(step, carry):
        received, made = carry
        index = jnp.clip(step - section, 0, micro - 1)
        where = jnp.stack([index, section]).astype(jnp.int32)
        packets, state = dispatch(where, hidden_in, received, routes[0], norm_gain)
        arrived = exchange(packets)
        produced = experts(arrived, w_gate[0], w_up[0], w_down[0])
        returned = exchange(produced)
        updated = combine(where, returned, state, routes[0], gate_probs[0])
        made = lax.dynamic_update_index_in_dim(made, updated, step, 0)
        received = lax.ppermute(updated, "pipe", [(s, s + 1) for s in range(stages - 1)])
        return received, made

    steps = micro + stages - 1
    start = (jnp.zeros((tokens, width), BF16), jnp.zeros((steps, tokens, width), BF16))
    received, made = lax.fori_loop(0, steps, advance, start)
    saved = lax.dynamic_slice_in_dim(made, section, micro, 0)
    return saved[None]


def solution(mesh):
    in_specs = (
        P(None, GROUP, None),
        P("pipe", None, GROUP, None),
        P("pipe", None, GROUP, None),
        P("pipe", None),
        P("pipe", GROUP, None, None),
        P("pipe", GROUP, None, None),
        P("pipe", GROUP, None, None),
    )
    out_specs = P("pipe", None, GROUP, None)
    return jax.shard_map(on_device, mesh=mesh, in_specs=in_specs, out_specs=out_specs, check_vma=False)
```

time: 813 us -> 571 us (0.70)
  local copies, waits for them, and re-layouts: 250 us -> 17 us
  Pallas kernels: 0 us -> 130 us
  matrix products: 110 us -> 0 us
  other arithmetic: 30.6 us -> 4.11 us
    scatter x7 -> x0, local copies, waits for them, and re-layouts: 156 us -> none  [layer(): outgoing.at[chosen, slots].set(jnp.repeat(normed, top_count, axis=0))]
    pallas_call x0 -> x21, Pallas kernels: none -> 130 us  [the longest x7 87.5 us: advance(): produced = experts(arrived, w_gate[0], w_up[0], w_down[0])]
    dot_general x21 -> x0, matrix products: 110 us -> none  [the longest x7 62.3 us: expert_block(): jnp.einsum('nlcf,lfd->nlcd', hidden, wdown, preferred_element_type=jnp.fl...]
    gather x7 -> x0, local copies, waits for them, and re-layouts: 30.1 us -> none  [layer(): results = returned.reshape(experts, capacity, width)[chosen, slots]]
    reshape x35 -> x0, local copies, waits for them, and re-layouts: 25 us -> none  [the longest x14 18.8 us: layer(): grouped = outgoing.reshape(groups, local_experts, capacity, width)]
    convert_element_type x7 -> x0, local copies, waits for them, and re-layouts: 19.5 us -> none  [expert_block(): jnp.einsum('nlcf,lfd->nlcd', hidden, wdown, preferred_element_type=jnp.fl...]
    select_n x7 -> x0, other arithmetic: 11.8 us -> none  [advance(): jnp.where(valid, lax.dynamic_update_index_in_dim(saved, updated, clipped,...]
    while x14 -> x16, local copies, waits for them, and re-layouts: 0.03 us -> 9.69 us
  transfers between devices with their start and end apart: 14 -> 14, of which waited for: 14 -> 14; matrix products, arithmetic and copies ran while one was open for 0% -> 1% of each run, Pallas kernels for 0% -> 0%
where the time goes in v1:
time: 571 us; the launch traced here: 569 us
  blocking collectives  203 us (36%)
  waiting for transfers between devices  165 us (29%)
  Pallas kernels  130 us (23%)
  starting transfers between devices  50.1 us (9%)
  local copies, waits for them, and re-layouts  17 us (3%)
    all_to_all x7, blocking collectives, exchange(): lax.all_to_all(packets, GROUP, split_axis=0, concat_axis=0, tiled=True)  203 us
    all_to_all x7, waiting for transfers between devices, exchange(): lax.all_to_all(packets, GROUP, split_axis=0, concat_axis=0, tiled=True)  155 us
    pallas_call x7, Pallas kernels, advance(): produced = experts(arrived, w_gate[0], w_up[0], w_down[0])  87.5 us
    all_to_all x7, starting transfers between devices, exchange(): lax.all_to_all(packets, GROUP, split_axis=0, concat_axis=0, tiled=True)  31.3 us
    pallas_call x7, Pallas kernels, advance(): packets, state = dispatch(where, hidden_in, received, routes[0], norm_gain)  22.8 us
    pallas_call x7, Pallas kernels, advance(): updated = combine(where, returned, state, routes[0], gate_probs[0])  19.8 us
    ppermute x7, starting transfers between devices, advance(): lax.ppermute(updated, 'pipe', [(s, s + 1) for s in range(stages - 1)])  18.8 us
  transfers between devices with their start and end apart: 14, of which 14 were waited for; matrix products, arithmetic and copies ran while one was open for 1% of the time, Pallas kernels for 0%

profile of v1, /device:TPU:1, one launch (start us, length us, event | category | flops | bytes accessed | tf_op | source)
XLA Modules:
  0.0 569.4 jit_solution(18003241067198614012)
XLA Ops:
  1.6 566.9 %while.15 = (s32[]{:T(128)}, bf16[32,2048]{1,0:T(8,128)(2,1)S(1)}, bf16[7,32,2048]{2,1,0:T(8,128)(2,1)S(1)}, s32[]{:T(128)}, s32[1,4,32,8]{3,2,1,0:T(8,128)S(1)}...) while((s32[]{:T(128)}, bf16[32,2048]{1,0:T(8,128)(2,1)S(1)}, ...), condition=%wide.region_1.2_spmd, body=%wide.region_0.1_spmd.sunk | while | flops 7 | bytes 14942505 | solution.py:233
  2.2 3.3 dispatch.5
  5.5 31.8 %all_to_all.20 = bf16[32,8,3072]{2,1,0:T(8,128)(2,1)S(1)} all-to-all(bf16[32,8,3072]{2,1,0:T(8,128)(2,1)} %bitcast.44), channel_id=1, replica_groups=mesh['pipe'=4,'exp'=16,'pair'=2] {'exp','pair'}, dimensions={0} | all-to-all | bytes 3145728 | tf_op jit(solution)/shard_map/while/body/eval_jaxpr/all_to_all | solution.py:216
  37.3 12.5 %experts.5 = bf16[256,3072]{1,0:T(8,128)(2,1)} custom-call(bf16[256,3072]{1,0:T(8,128)(2,1)S(1)} %bitcast.39, bf16[2,2048,768]{2,1,0:T(8,128)(2,1)} %bitcast.41, bf16[2,2048,768]{2,1,0:T(8,128)(2,1)} %bitcast.42, bf16[2,768,2048]{2,1,0:T(8,128)(2,1)} %bitcast.43), custom_call_target="tpu_custom_call" | custom-call | tf_op jit(solution)/shard_map/while/body/eval_jaxpr/experts/pallas_call | solution.py:224
  49.8 4.4 all-to-all-start.1
  54.2 21.0 %all-to-all-done.1 = bf16[32,8,3072]{2,1,0:T(8,128)(2,1)S(1)} async-done(((bf16[32,8,3072]{2,1,0:T(8,128)(2,1)}), bf16[32,8,3072]{2,1,0:T(8,128)(2,1)S(1)}, u32[]{:S(2)}, u32[]{:S(2)}) %all-to-all-start.1) | async-done | bytes 1572896 | tf_op jit(solution)/shard_map/while/body/eval_jaxpr/all_to_all | solution.py:216
  76.4 2.8 combine.5
  79.2 7.3 %collective-permute-start = (bf16[32,2048]{1,0:T(8,128)(2,1)}, bf16[32,2048]{1,0:T(8,128)(2,1)S(1)}, u32[]{:S(2)}, u32[]{:S(2)}) collective-permute-start(bf16[32,2048]{1,0:T(8,128)(2,1)} %combine.5), channel_id=1, source_target_pairs={{0,32},{32,64},{64,96},{1,33},{33,65},{65,97},{2,34},{34,66},{66,9... | collective-permute-start | bytes 393224 | tf_op jit(solution)/shard_map/while/body/eval_jaxpr/ppermute | solution.py:228
  89.4 3.3 dispatch.5
  92.6 25.1 %all_to_all.20 = bf16[32,8,3072]{2,1,0:T(8,128)(2,1)S(1)} all-to-all(bf16[32,8,3072]{2,1,0:T(8,128)(2,1)} %bitcast.44), channel_id=1, replica_groups=mesh['pipe'=4,'exp'=16,'pair'=2] {'exp','pair'}, dimensions={0} | all-to-all | bytes 3145728 | tf_op jit(solution)/shard_map/while/body/eval_jaxpr/all_to_all | solution.py:216
  117.7 12.5 %experts.5 = bf16[256,3072]{1,0:T(8,128)(2,1)} custom-call(bf16[256,3072]{1,0:T(8,128)(2,1)S(1)} %bitcast.39, bf16[2,2048,768]{2,1,0:T(8,128)(2,1)} %bitcast.41, bf16[2,2048,768]{2,1,0:T(8,128)(2,1)} %bitcast.42, bf16[2,768,2048]{2,1,0:T(8,128)(2,1)} %bitcast.43), custom_call_target="tpu_custom_call" | custom-call | tf_op jit(solution)/shard_map/while/body/eval_jaxpr/experts/pallas_call | solution.py:224
  130.2 4.0 all-to-all-start.1
  134.2 22.4 %all-to-all-done.1 = bf16[32,8,3072]{2,1,0:T(8,128)(2,1)S(1)} async-done(((bf16[32,8,3072]{2,1,0:T(8,128)(2,1)}), bf16[32,8,3072]{2,1,0:T(8,128)(2,1)S(1)}, u32[]{:S(2)}, u32[]{:S(2)}) %all-to-all-start.1) | async-done | bytes 1572896 | tf_op jit(solution)/shard_map/while/body/eval_jaxpr/all_to_all | solution.py:216
  157.8 2.8 combine.5
  165.4 3.3 dispatch.5
  168.6 28.6 %all_to_all.20 = bf16[32,8,3072]{2,1,0:T(8,128)(2,1)S(1)} all-to-all(bf16[32,8,3072]{2,1,0:T(8,128)(2,1)} %bitcast.44), channel_id=1, replica_groups=mesh['pipe'=4,'exp'=16,'pair'=2] {'exp','pair'}, dimensions={0} | all-to-all | bytes 3145728 | tf_op jit(solution)/shard_map/while/body/eval_jaxpr/all_to_all | solution.py:216
  197.2 12.5 %experts.5 = bf16[256,3072]{1,0:T(8,128)(2,1)} custom-call(bf16[256,3072]{1,0:T(8,128)(2,1)S(1)} %bitcast.39, bf16[2,2048,768]{2,1,0:T(8,128)(2,1)} %bitcast.41, bf16[2,2048,768]{2,1,0:T(8,128)(2,1)} %bitcast.42, bf16[2,768,2048]{2,1,0:T(8,128)(2,1)} %bitcast.43), custom_call_target="tpu_custom_call" | custom-call | tf_op jit(solution)/shard_map/while/body/eval_jaxpr/experts/pallas_call | solution.py:224
  209.7 4.6 all-to-all-start.1
  214.3 22.4 %all-to-all-done.1 = bf16[32,8,3072]{2,1,0:T(8,128)(2,1)S(1)} async-done(((bf16[32,8,3072]{2,1,0:T(8,128)(2,1)}), bf16[32,8,3072]{2,1,0:T(8,128)(2,1)S(1)}, u32[]{:S(2)}, u32[]{:S(2)}) %all-to-all-start.1) | async-done | bytes 1572896 | tf_op jit(solution)/shard_map/while/body/eval_jaxpr/all_to_all | solution.py:216
  237.9 2.8 combine.5
  240.7 1.9 collective-permute-start
  245.5 3.3 dispatch.5
  248.7 29.6 %all_to_all.20 = bf16[32,8,3072]{2,1,0:T(8,128)(2,1)S(1)} all-to-all(bf16[32,8,3072]{2,1,0:T(8,128)(2,1)} %bitcast.44), channel_id=1, replica_groups=mesh['pipe'=4,'exp'=16,'pair'=2] {'exp','pair'}, dimensions={0} | all-to-all | bytes 3145728 | tf_op jit(solution)/shard_map/while/body/eval_jaxpr/all_to_all | solution.py:216
  278.4 12.5 %experts.5 = bf16[256,3072]{1,0:T(8,128)(2,1)} custom-call(bf16[256,3072]{1,0:T(8,128)(2,1)S(1)} %bitcast.39, bf16[2,2048,768]{2,1,0:T(8,128)(2,1)} %bitcast.41, bf16[2,2048,768]{2,1,0:T(8,128)(2,1)} %bitcast.42, bf16[2,768,2048]{2,1,0:T(8,128)(2,1)} %bitcast.43), custom_call_target="tpu_custom_call" | custom-call | tf_op jit(solution)/shard_map/while/body/eval_jaxpr/experts/pallas_call | solution.py:224
  290.9 4.3 all-to-all-start.1
  295.2 22.4 %all-to-all-done.1 = bf16[32,8,3072]{2,1,0:T(8,128)(2,1)S(1)} async-done(((bf16[32,8,3072]{2,1,0:T(8,128)(2,1)}), bf16[32,8,3072]{2,1,0:T(8,128)(2,1)S(1)}, u32[]{:S(2)}, u32[]{:S(2)}) %all-to-all-start.1) | async-done | bytes 1572896 | tf_op jit(solution)/shard_map/while/body/eval_jaxpr/all_to_all | solution.py:216
  318.8 2.8 combine.5
  321.6 1.9 collective-permute-start
  326.4 3.3 dispatch.5
  329.6 29.4 %all_to_all.20 = bf16[32,8,3072]{2,1,0:T(8,128)(2,1)S(1)} all-to-all(bf16[32,8,3072]{2,1,0:T(8,128)(2,1)} %bitcast.44), channel_id=1, replica_groups=mesh['pipe'=4,'exp'=16,'pair'=2] {'exp','pair'}, dimensions={0} | all-to-all | bytes 3145728 | tf_op jit(solution)/shard_map/while/body/eval_jaxpr/all_to_all | solution.py:216
  359.0 12.5 %experts.5 = bf16[256,3072]{1,0:T(8,128)(2,1)} custom-call(bf16[256,3072]{1,0:T(8,128)(2,1)S(1)} %bitcast.39, bf16[2,2048,768]{2,1,0:T(8,128)(2,1)} %bitcast.41, bf16[2,2048,768]{2,1,0:T(8,128)(2,1)} %bitcast.42, bf16[2,768,2048]{2,1,0:T(8,128)(2,1)} %bitcast.43), custom_call_target="tpu_custom_call" | custom-call | tf_op jit(solution)/shard_map/while/body/eval_jaxpr/experts/pallas_call | solution.py:224
  371.5 4.6 all-to-all-start.1
  376.2 22.4 %all-to-all-done.1 = bf16[32,8,3072]{2,1,0:T(8,128)(2,1)S(1)} async-done(((bf16[32,8,3072]{2,1,0:T(8,128)(2,1)}), bf16[32,8,3072]{2,1,0:T(8,128)(2,1)S(1)}, u32[]{:S(2)}, u32[]{:S(2)}) %all-to-all-start.1) | async-done | bytes 1572896 | tf_op jit(solution)/shard_map/while/body/eval_jaxpr/all_to_all | solution.py:216
  399.7 2.8 combine.5
  402.5 1.9 collective-permute-start
  407.3 3.3 dispatch.5
  410.6 29.4 %all_to_all.20 = bf16[32,8,3072]{2,1,0:T(8,128)(2,1)S(1)} all-to-all(bf16[32,8,3072]{2,1,0:T(8,128)(2,1)} %bitcast.44), channel_id=1, replica_groups=mesh['pipe'=4,'exp'=16,'pair'=2] {'exp','pair'}, dimensions={0} | all-to-all | bytes 3145728 | tf_op jit(solution)/shard_map/while/body/eval_jaxpr/all_to_all | solution.py:216
  439.9 12.5 %experts.5 = bf16[256,3072]{1,0:T(8,128)(2,1)} custom-call(bf16[256,3072]{1,0:T(8,128)(2,1)S(1)} %bitcast.39, bf16[2,2048,768]{2,1,0:T(8,128)(2,1)} %bitcast.41, bf16[2,2048,768]{2,1,0:T(8,128)(2,1)} %bitcast.42, bf16[2,768,2048]{2,1,0:T(8,128)(2,1)} %bitcast.43), custom_call_target="tpu_custom_call" | custom-call | tf_op jit(solution)/shard_map/while/body/eval_jaxpr/experts/pallas_call | solution.py:224
  452.4 4.6 all-to-all-start.1
  457.1 22.4 %all-to-all-done.1 = bf16[32,8,3072]{2,1,0:T(8,128)(2,1)S(1)} async-done(((bf16[32,8,3072]{2,1,0:T(8,128)(2,1)}), bf16[32,8,3072]{2,1,0:T(8,128)(2,1)S(1)}, u32[]{:S(2)}, u32[]{:S(2)}) %all-to-all-start.1) | async-done | bytes 1572896 | tf_op jit(solution)/shard_map/while/body/eval_jaxpr/all_to_all | solution.py:216
  480.6 2.8 combine.5
  483.5 1.9 collective-permute-start
  488.2 3.3 dispatch.5
  491.5 29.4 %all_to_all.20 = bf16[32,8,3072]{2,1,0:T(8,128)(2,1)S(1)} all-to-all(bf16[32,8,3072]{2,1,0:T(8,128)(2,1)} %bitcast.44), channel_id=1, replica_groups=mesh['pipe'=4,'exp'=16,'pair'=2] {'exp','pair'}, dimensions={0} | all-to-all | bytes 3145728 | tf_op jit(solution)/shard_map/while/body/eval_jaxpr/all_to_all | solution.py:216
  520.8 12.5 %experts.5 = bf16[256,3072]{1,0:T(8,128)(2,1)} custom-call(bf16[256,3072]{1,0:T(8,128)(2,1)S(1)} %bitcast.39, bf16[2,2048,768]{2,1,0:T(8,128)(2,1)} %bitcast.41, bf16[2,2048,768]{2,1,0:T(8,128)(2,1)} %bitcast.42, bf16[2,768,2048]{2,1,0:T(8,128)(2,1)} %bitcast.43), custom_call_target="tpu_custom_call" | custom-call | tf_op jit(solution)/shard_map/while/body/eval_jaxpr/experts/pallas_call | solution.py:224
  533.3 4.6 all-to-all-start.1
  538.0 22.4 %all-to-all-done.1 = bf16[32,8,3072]{2,1,0:T(8,128)(2,1)S(1)} async-done(((bf16[32,8,3072]{2,1,0:T(8,128)(2,1)}), bf16[32,8,3072]{2,1,0:T(8,128)(2,1)S(1)}, u32[]{:S(2)}, u32[]{:S(2)}) %all-to-all-start.1) | async-done | bytes 1572896 | tf_op jit(solution)/shard_map/while/body/eval_jaxpr/all_to_all | solution.py:216
  561.5 2.8 combine.5
  (42 shorter events, 34.1 us)
Async XLA Ops:
  49.8 25.4 %all-to-all-start.1 = ((bf16[32,8,3072]{2,1,0:T(8,128)(2,1)}), bf16[32,8,3072]{2,1,0:T(8,128)(2,1)S(1)}, u32[]{:S(2)}, u32[]{:S(2)}) async-start(bf16[32,8,3072]{2,1,0:T(8,128)(2,1)} %bitcast.36), calls=%async_computation.1 | async-start | bytes 3145728 | tf_op jit(solution)/shard_map/while/body/eval_jaxpr/all_to_all | solution.py:216
  75.2 1.2 copy-start
  79.2 9.6 %collective-permute-start = (bf16[32,2048]{1,0:T(8,128)(2,1)}, bf16[32,2048]{1,0:T(8,128)(2,1)S(1)}, u32[]{:S(2)}, u32[]{:S(2)}) collective-permute-start(bf16[32,2048]{1,0:T(8,128)(2,1)} %combine.5), channel_id=1, source_target_pairs={{0,32},{32,64},{64,96},{1,33},{33,65},{65,97},{2,34},{34,66},{66,9... | collective-permute-start | bytes 393224 | tf_op jit(solution)/shard_map/while/body/eval_jaxpr/ppermute | solution.py:228
  130.2 26.4 %all-to-all-start.1 = ((bf16[32,8,3072]{2,1,0:T(8,128)(2,1)}), bf16[32,8,3072]{2,1,0:T(8,128)(2,1)S(1)}, u32[]{:S(2)}, u32[]{:S(2)}) async-start(bf16[32,8,3072]{2,1,0:T(8,128)(2,1)} %bitcast.36), calls=%async_computation.1 | async-start | bytes 3145728 | tf_op jit(solution)/shard_map/while/body/eval_jaxpr/all_to_all | solution.py:216
  156.6 1.2 copy-start
  160.6 4.2 collective-permute-start
  209.7 27.0 %all-to-all-start.1 = ((bf16[32,8,3072]{2,1,0:T(8,128)(2,1)}), bf16[32,8,3072]{2,1,0:T(8,128)(2,1)S(1)}, u32[]{:S(2)}, u32[]{:S(2)}) async-start(bf16[32,8,3072]{2,1,0:T(8,128)(2,1)} %bitcast.36), calls=%async_computation.1 | async-start | bytes 3145728 | tf_op jit(solution)/shard_map/while/body/eval_jaxpr/all_to_all | solution.py:216
  236.7 1.2 copy-start
  240.7 4.2 collective-permute-start
  290.9 26.8 %all-to-all-start.1 = ((bf16[32,8,3072]{2,1,0:T(8,128)(2,1)}), bf16[32,8,3072]{2,1,0:T(8,128)(2,1)S(1)}, u32[]{:S(2)}, u32[]{:S(2)}) async-start(bf16[32,8,3072]{2,1,0:T(8,128)(2,1)} %bitcast.36), calls=%async_computation.1 | async-start | bytes 3145728 | tf_op jit(solution)/shard_map/while/body/eval_jaxpr/all_to_all | solution.py:216
  317.6 1.2 copy-start
  321.6 4.2 collective-permute-start
  371.5 27.0 %all-to-all-start.1 = ((bf16[32,8,3072]{2,1,0:T(8,128)(2,1)}), bf16[32,8,3072]{2,1,0:T(8,128)(2,1)S(1)}, u32[]{:S(2)}, u32[]{:S(2)}) async-start(bf16[32,8,3072]{2,1,0:T(8,128)(2,1)} %bitcast.36), calls=%async_computation.1 | async-start | bytes 3145728 | tf_op jit(solution)/shard_map/while/body/eval_jaxpr/all_to_all | solution.py:216
  398.6 1.2 copy-start
  402.5 4.2 collective-permute-start
  452.4 27.0 %all-to-all-start.1 = ((bf16[32,8,3072]{2,1,0:T(8,128)(2,1)}), bf16[32,8,3072]{2,1,0:T(8,128)(2,1)S(1)}, u32[]{:S(2)}, u32[]{:S(2)}) async-start(bf16[32,8,3072]{2,1,0:T(8,128)(2,1)} %bitcast.36), calls=%async_computation.1 | async-start | bytes 3145728 | tf_op jit(solution)/shard_map/while/body/eval_jaxpr/all_to_all | solution.py:216
  479.5 1.2 copy-start
  483.5 4.2 collective-permute-start
  533.3 27.0 %all-to-all-start.1 = ((bf16[32,8,3072]{2,1,0:T(8,128)(2,1)}), bf16[32,8,3072]{2,1,0:T(8,128)(2,1)S(1)}, u32[]{:S(2)}, u32[]{:S(2)}) async-start(bf16[32,8,3072]{2,1,0:T(8,128)(2,1)} %bitcast.36), calls=%async_computation.1 | async-start | bytes 3145728 | tf_op jit(solution)/shard_map/while/body/eval_jaxpr/all_to_all | solution.py:216
  560.4 1.2 copy-start
  564.4 4.2 collective-permute-start

commit v2 on v1

v2 whole, which is shorter than its diff:
```python
import functools

import jax
import jax.numpy as jnp
from jax import lax
from jax.experimental import pallas as pl
from jax.experimental.pallas import tpu as pltpu
from jax.sharding import PartitionSpec as P

EPS = 1e-06
F32 = jnp.float32
BF16 = jnp.bfloat16
GROUP = ("exp", "pair")


def dot(a, b):
    return jnp.dot(a, b, preferred_element_type=F32)


def dot_nt(a, b):
    return lax.dot_general(a, b, (((1,), (1,)), ((), ())), preferred_element_type=F32)


def iota(shape, dim):
    return lax.broadcasted_iota(jnp.int32, shape, dim)


def select_matrix(shape, source):
    return jnp.where(iota(shape, 1) == source(iota(shape, 0)), 1.0, 0.0).astype(BF16)


def naming(chosen, experts, values=None):
    tokens, top = chosen.shape
    ids = iota((tokens, experts), 1)
    total = jnp.zeros((tokens, experts), F32)
    for k in range(top):
        value = 1.0 if values is None else values[:, k : k + 1]
        total = total + jnp.where(chosen[:, k : k + 1] == ids, value, 0.0)
    return total


def rank_of(named, block):
    tokens = named.shape[0]
    row, col = iota((tokens, tokens), 0), iota((tokens, tokens), 1)
    earlier = jnp.where((col < row) & (col // block == row // block), 1.0, 0.0)
    return dot(earlier.astype(BF16), named.astype(BF16))


def whole_slots(i):
    return (i >> 3) & 1, (i >> 2) & 1, i & 3


def half_slots(i):
    return (i >> 2) & 1, (i >> 1) & 1, 4 + (i & 1)


def spread_of(rows, experts, side, slots):
    return select_matrix((rows, experts), lambda i: 4 * (i >> 4) + 2 * side + slots(i)[0])


def dispatch_kernel(
    where_ref, hidden_ref, other_ref, same_ref, cross_ref, routes_ref, routes_other_ref, gain_ref, out_ref, state_ref, *, experts
):
    index, section, side = where_ref[0], where_ref[1], where_ref[2]
    rows = out_ref.shape[0]
    tokens = hidden_ref.shape[1]
    width = state_ref.shape[1]
    half = width // 2
    same, cross = same_ref[...].astype(F32), cross_ref[...].astype(F32)
    mine = jnp.where(section == 0, hidden_ref[index], (same[:tokens] + cross[tokens:]).astype(BF16))
    others = jnp.where(section == 0, other_ref[index], (same[tokens:] + cross[:tokens]).astype(BF16))
    state = jnp.concatenate([mine, others], axis=0)
    state_ref[...] = state
    floated = state.astype(F32)
    scale = lax.rsqrt(jnp.mean(floated * floated, axis=-1, keepdims=True) + EPS)
    normed = (floated * scale * gain_ref[...]).astype(BF16)
    named = naming(jnp.concatenate([routes_ref[index], routes_other_ref[index]], axis=0), experts)
    rank = rank_of(named, tokens).astype(BF16)
    named = named.astype(BF16)

    def pick(slots):
        spread = spread_of(rows, experts, side, slots)
        named_rows = dot_nt(spread, named)
        rank_rows = dot_nt(spread, rank).astype(jnp.int32)
        row, col = iota(rank_rows.shape, 0), iota(rank_rows.shape, 1)
        _, block, slot = slots(row)
        return jnp.where((col // tokens == block) & (rank_rows == slot), named_rows, 0.0), row

    whole, _ = pick(whole_slots)
    out_ref[:, :width] = dot(whole.astype(BF16), normed).astype(BF16)
    rest, row = pick(half_slots)
    first = ((row >> 3) & 1) == 0
    left = jnp.where(first, rest, 0.0).astype(BF16)
    right = jnp.where(first, 0.0, rest).astype(BF16)
    out_ref[:, width:] = (dot(left, normed[:, :half]) + dot(right, normed[:, half:])).astype(BF16)


def combine_kernel(
    where_ref, returned_ref, state_ref, routes_ref, routes_other_ref, probs_ref, probs_other_ref, part_ref, *, experts
):
    index, side = where_ref[0], where_ref[2]
    rows = returned_ref.shape[0]
    both, width = state_ref.shape
    tokens = both // 2
    half = width // 2
    chosen = jnp.concatenate([routes_ref[index], routes_other_ref[index]], axis=0)
    probs = jnp.concatenate([probs_ref[index], probs_other_ref[index]], axis=0)
    weights = probs / jnp.sum(probs, axis=-1, keepdims=True)
    rank = rank_of(naming(chosen, experts), tokens).astype(BF16)
    weight = naming(chosen, experts, weights)
    high = weight.astype(BF16)
    low = (weight - high.astype(F32)).astype(BF16)

    def pick(slots):
        spread = spread_of(rows, experts, side, slots)
        rank_x = dot_nt(rank, spread).astype(jnp.int32)
        row, col = iota(rank_x.shape, 0), iota(rank_x.shape, 1)
        _, block, slot = slots(col)
        held = (row // tokens == block) & (rank_x == slot)
        return [jnp.where(held, dot_nt(part, spread), 0.0) for part in (high, low)], col

    whole, _ = pick(whole_slots)
    sums = dot(jnp.concatenate(whole, axis=0).astype(BF16), returned_ref[:, :width])
    rest, col = pick(half_slots)
    first = ((col >> 3) & 1) == 0
    halves = [jnp.where(first, part, 0.0) for part in rest] + [jnp.where(first, 0.0, part) for part in rest]
    tail = dot(jnp.concatenate(halves, axis=0).astype(BF16), returned_ref[:, width:])
    mixed = sums[:both] + sums[both:]
    mixed_left = tail[:both] + tail[both : 2 * both]
    mixed_right = tail[2 * both : 3 * both] + tail[3 * both :]
    shared = state_ref[...].astype(F32) * 0.5
    part_ref[:, :half] = (shared[:, :half] + mixed[:, :half] + mixed_left).astype(BF16)
    part_ref[:, half:] = (shared[:, half:] + mixed[:, half:] + mixed_right).astype(BF16)


def expert_kernel(
    arrived_ref, gate_hbm, up_hbm, down_hbm, out_ref, gate_v, up_v, down_v, rows_v, rest_v, mid_v, made_v, sems, *, cuts
):
    local, width, hidden = gate_v.shape
    sources = arrived_ref.shape[0] // 16
    half = width // 2
    cut = hidden // cuts
    full = 8 * sources

    def copies(e, f):
        part = pl.ds(f * cut, cut)
        return (
            pltpu.make_async_copy(gate_hbm.at[e, :, part], gate_v.at[e, :, part], sems.at[0, e, f]),
            pltpu.make_async_copy(up_hbm.at[e, :, part], up_v.at[e, :, part], sems.at[1, e, f]),
        )

    def down_copy(e, f):
        part = pl.ds(f * cut, cut)
        return pltpu.make_async_copy(down_hbm.at[e, part, :], down_v.at[e, part, :], sems.at[2, e, f])

    for e in range(local):
        for f in range(cuts):
            for copy in copies(e, f):
                copy.start()
        for f in range(cuts):
            down_copy(e, f).start()
    for g in range(sources):
        for e in range(local):
            rows_v[e, 8 * g : 8 * g + 8] = arrived_ref[16 * g + 8 * e : 16 * g + 8 * e + 8, :width]
        for q in range(2):
            rest_v[8 * g : 8 * g + 8, q * half : (q + 1) * half] = arrived_ref[16 * g + 8 * q : 16 * g + 8 * q + 8, width:]
    for e in range(local):
        pick = select_matrix((4 * sources, full), lambda i: 8 * (i >> 2) + 4 * e + (i & 3))
        rows_v[e, full:] = dot(pick, rest_v[...]).astype(BF16)
    for e in range(local):
        for f in range(cuts):
            gate_copy, up_copy = copies(e, f)
            part = slice(f * cut, (f + 1) * cut)
            gate_copy.wait()
            gate = dot(rows_v[e], gate_v[e, :, part])
            up_copy.wait()
            upward = dot(rows_v[e], up_v[e, :, part])
            mid_v[:, part] = (jax.nn.silu(gate) * upward).astype(BF16)
        for f in range(cuts):
            down_copy(e, f).wait()
        product = dot(mid_v[...], down_v[e]).astype(BF16)
        made_v[e] = product[full:]
        for g in range(sources):
            out_ref[16 * g + 8 * e : 16 * g + 8 * e + 8, :width] = product[8 * g : 8 * g + 8]
    shape = (full, full)
    target, column = iota(shape, 0), iota(shape, 1)
    source = ((target >> 2) & 1) * (4 * sources) + 4 * (target >> 3) + (target & 3)
    place = jnp.where(column == source, 1.0, 0.0).astype(BF16)
    rest = dot(place, made_v[...].reshape(full, width)).astype(BF16)
    for g in range(sources):
        for q in range(2):
            out_ref[16 * g + 8 * q : 16 * g + 8 * q + 8, width:] = rest[8 * g : 8 * g + 8, q * half : (q + 1) * half]


def on_device(hidden_in, routes, gate_probs, norm_gain, w_gate, w_up, w_down):
    section = lax.axis_index("pipe")
    side = lax.axis_index("pair")
    stages = lax.axis_size("pipe")
    micro, tokens, width = hidden_in.shape
    groups = lax.axis_size(("exp", "pair"))
    local, hidden = w_gate.shape[1], w_gate.shape[3]
    top = routes.shape[3]
    assert local == 2 and lax.axis_size("pair") == 2 and top * tokens == 4 * local * groups
    smem = pl.BlockSpec(memory_space=pltpu.SMEM)
    vmem = pl.BlockSpec(memory_space=pltpu.VMEM)
    hbm = pl.BlockSpec(memory_space=pl.ANY)
    packet = jax.ShapeDtypeStruct((8 * groups, width + width // 2), BF16)
    token_rows = jax.ShapeDtypeStruct((2 * tokens, width), BF16)
    cuts = 3

    dispatch = pl.pallas_call(
        functools.partial(dispatch_kernel, experts=local * groups),
        out_shape=(packet, token_rows),
        in_specs=[smem] + [vmem] * 7,
        out_specs=(vmem, vmem),
        compiler_params=pltpu.CompilerParams(vmem_limit_bytes=16 * 2**20),
        name="dispatch",
    )
    experts = pl.pallas_call(
        functools.partial(expert_kernel, cuts=cuts),
        out_shape=packet,
        in_specs=[vmem, hbm, hbm, hbm],
        out_specs=vmem,
        scratch_shapes=[
            pltpu.VMEM((local, width, hidden), BF16),
            pltpu.VMEM((local, width, hidden), BF16),
            pltpu.VMEM((local, hidden, width), BF16),
            pltpu.VMEM((local, 6 * groups, width), BF16),
            pltpu.VMEM((4 * groups, width), BF16),
            pltpu.VMEM((6 * groups, hidden), BF16),
            pltpu.VMEM((local, 2 * groups, width), BF16),
            pltpu.SemaphoreType.DMA((3, local, cuts)),
        ],
        compiler_params=pltpu.CompilerParams(vmem_limit_bytes=32 * 2**20),
        name="experts",
    )
    combine = pl.pallas_call(
        functools.partial(combine_kernel, experts=local * groups),
        out_shape=token_rows,
        in_specs=[smem] + [vmem] * 6,
        out_specs=vmem,
        compiler_params=pltpu.CompilerParams(vmem_limit_bytes=16 * 2**20),
        name="combine",
    )

    def exchange(packets):
        return lax.all_to_all(packets, "exp", split_axis=0, concat_axis=0, tiled=True)

    swap = [(0, 1), (1, 0)]
    stage_pair = ("pipe", "pair")
    hidden_other = lax.ppermute(hidden_in, stage_pair, swap)
    routes_other = lax.ppermute(routes[0], "pair", swap)
    probs_other = lax.ppermute(gate_probs[0], "pair", swap)
    onward = [(2 * s + y, 2 * s + 2 + y) for s in range(stages - 1) for y in range(2)]
    across = [(2 * s + y, 2 * s + 3 - y) for s in range(stages - 1) for y in range(2)]

    def advance(step, carry):
        same, cross, made = carry
        index = jnp.clip(step - section, 0, micro - 1)
        where = jnp.stack([index, section, side]).astype(jnp.int32)

        def layer():
            packets, state = dispatch(
                where, hidden_in, hidden_other, same, cross, routes[0], routes_other, norm_gain
            )
            produced = experts(exchange(packets), w_gate[0], w_up[0], w_down[0])
            return combine(
                where, exchange(produced), state, routes[0], routes_other, gate_probs[0], probs_other
            )

        part = lax.cond((step >= section) & (step < section + micro), layer, lambda: same)
        made = lax.dynamic_update_index_in_dim(made, part, step, 0)
        same = lax.ppermute(part, stage_pair, onward)
        cross = lax.ppermute(part, stage_pair, across)
        return same, cross, made

    steps = micro + stages - 1
    blank = jnp.zeros((2 * tokens, width), BF16)
    start = (blank, blank, jnp.zeros((steps, 2 * tokens, width), BF16))
    same, cross, made = lax.fori_loop(0, steps, advance, start)
    own = lax.dynamic_slice(made, (section, 0, 0), (micro, tokens, width))
    given = lax.dynamic_slice(made, (section, tokens, 0), (micro, tokens, width))
    taken = lax.ppermute(given, "pair", swap)
    return (own.astype(F32) + taken.astype(F32)).astype(BF16)[None]


def solution(mesh):
    in_specs = (
        P(None, GROUP, None),
        P("pipe", None, GROUP, None),
        P("pipe", None, GROUP, None),
        P("pipe", None),
        P("pipe", GROUP, None, None),
        P("pipe", GROUP, None, None),
        P("pipe", GROUP, None, None),
    )
    out_specs = P("pipe", None, GROUP, None)
    return jax.shard_map(on_device, mesh=mesh, in_specs=in_specs, out_specs=out_specs, check_vma=False)
```

time: 571 us -> 510 us (0.89)
  starting transfers between devices: 50.1 us -> 151 us
  Pallas kernels: 130 us -> 55.5 us
  waiting for transfers between devices: 165 us -> 106 us
  local copies, waits for them, and re-layouts: 17 us -> 1.95 us
  blocking collectives: 203 us -> 189 us
    all_to_all x7 -> x0, waiting for transfers between devices: 155 us -> none  [exchange(): lax.all_to_all(packets, GROUP, split_axis=0, concat_axis=0, tiled=True)]
    ppermute x7 -> x18, starting transfers between devices: 18.8 us -> 151 us  [the longest x7 88.2 us: advance(): same = lax.ppermute(part, stage_pair, onward)]
    ppermute x7 -> x18, waiting for transfers between devices: 9.2 us -> 106 us  [the longest x7 65.8 us: advance(): same = lax.ppermute(part, stage_pair, onward)]
    pallas_call x21 -> x12, Pallas kernels: 130 us -> 55.5 us  [the longest x4 39.8 us: layer(): produced = experts(exchange(packets), w_gate[0], w_up[0], w_down[0])]
    all_to_all x7 -> x0, starting transfers between devices: 31.3 us -> none  [exchange(): lax.all_to_all(packets, GROUP, split_axis=0, concat_axis=0, tiled=True)]
    all_to_all x7 -> x8, blocking collectives: 203 us -> 189 us  [exchange(): lax.all_to_all(packets, 'exp', split_axis=0, concat_axis=0, tiled=True)]
    while x16 -> x2, local copies, waits for them, and re-layouts: 9.69 us -> 1.59 us  [on_device(): same, cross, made = lax.fori_loop(0, steps, advance, start)]
    dynamic_update_slice x7, local copies, waits for them, and re-layouts: 6.47 us -> 0.15 us  [advance(): made = lax.dynamic_update_index_in_dim(made, part, step, 0)]
  transfers between devices with their start and end apart: 14 -> 18, of which waited for: 14 -> 16; matrix products, arithmetic and copies ran while one was open for 1% -> 0% of each run, Pallas kernels for 0% -> 0%
where the time goes in v2:
time: 510 us; the launch traced here: 505 us
  blocking collectives  189 us (37%)
  starting transfers between devices  151 us (30%)
  waiting for transfers between devices  106 us (21%)
  Pallas kernels  55.5 us (11%)
    all_to_all x8, blocking collectives, exchange(): lax.all_to_all(packets, 'exp', split_axis=0, concat_axis=0, tiled=True)  189 us
    ppermute x7, starting transfers between devices, advance(): same = lax.ppermute(part, stage_pair, onward)  88.2 us
    ppermute x7, waiting for transfers between devices, advance(): same = lax.ppermute(part, stage_pair, onward)  65.8 us
    ppermute x7, starting transfers between devices, advance(): cross = lax.ppermute(part, stage_pair, across)  60.1 us
    pallas_call x4, Pallas kernels, layer(): produced = experts(exchange(packets), w_gate[0], w_up[0], w_down[0])  39.8 us
    ppermute x7, waiting for transfers between devices, advance(): cross = lax.ppermute(part, stage_pair, across)  27.9 us
  transfers between devices with their start and end apart: 18, of which 16 were waited for; matrix products, arithmetic and copies ran while one was open for 0% of the time, Pallas kernels for 0%

profile of v2, /device:TPU:1, one launch (start us, length us, event | category | flops | bytes accessed | tf_op | source)
XLA Modules:
  0.0 505.3 jit_solution(5441048911601017387)
XLA Ops:
  1.5 2.2 collective-permute-start.3
  5.3 3.3 collective-permute-done.4
  8.7 487.6 %while.21 = (s32[]{:T(128)}, bf16[64,2048]{1,0:T(8,128)(2,1)S(1)}, bf16[64,2048]{1,0:T(8,128)(2,1)S(1)}, bf16[7,64,2048]{2,1,0:T(8,128)(2,1)S(1)}, s32[]{:T(128)...) while((s32[]{:T(128)}, bf16[64,2048]{1,0:T(8,128)(2,1)S(1)}, ...), condition=%wide.region_3.4_spmd, body=%wide.region_0.3_spmd.sunk | while | flops 15 | bytes 9437655 | solution.py:280
  8.8 5.5 %collective-permute-start = (bf16[64,2048]{1,0:T(8,128)(2,1)S(1)}, bf16[64,2048]{1,0:T(8,128)(2,1)S(1)}, u32[]{:S(2)}, u32[]{:S(2)}) collective-permute-start(bf16[64,2048]{1,0:T(8,128)(2,1)S(1)} %get-tuple-element.604), channel_id=1, source_target_pairs={{0,32},{1,33},{32,64},{33,65},{64,96},{65,97},{2,34},{3,35},{34,66... | collective-permute-start | bytes 786440 | tf_op jit(solution)/shard_map/while/body/eval_jaxpr/ppermute | solution.py:273
  14.3 1.9 collective-permute-start.1
  16.3 57.3 %collective-permute-done = bf16[64,2048]{1,0:T(8,128)(2,1)S(1)} collective-permute-done((bf16[64,2048]{1,0:T(8,128)(2,1)S(1)}, bf16[64,2048]{1,0:T(8,128)(2,1)S(1)}, u32[]{:S(2)}, u32[]{:S(2)}) %collective-permute-start) | collective-permute-done | bytes 262176 | tf_op jit(solution)/shard_map/while/body/eval_jaxpr/ppermute | solution.py:273
  73.6 4.8 collective-permute-done.1
  78.6 64.9 %conditional.2 = (bf16[64,2048]{1,0:T(8,128)(2,1)S(1)}) conditional(s32[]{:T(128)} %convert_element_type.30, bf16[64,2048]{1,0:T(8,128)(2,1)S(1)} %copy.20, (s32[1,4,32,8]{3,2,1,0:T(8,128)S(1)}, s32[3]{0:T(128)S(1)}, bf16[4,32,2048]{2,1,0:T(8,128)(2,1)}, bf16[4,32,2048]{2,1,0:T(8,128)(2,1)S(1)}, bf16[64,2048]{1,0:T(8,128)(2,1)S(1)}, ...), branch_computations={%region_1.1_spmd, %region_2.2_spmd} | conditional | bytes 6291464 | solution.py:271
  78.6 2.3 dispatch.1
  80.9 26.2 %all_to_all.16 = bf16[16,16,3072]{2,1,0:T(8,128)(2,1)S(1)} all-to-all(bf16[16,16,3072]{2,1,0:T(8,128)(2,1)S(1)} %bitcast.29), channel_id=1, replica_groups=mesh['pipe'=4,'exp'=16,'pair'=2] {'exp'}, dimensions={0} | all-to-all | bytes 3145728 | tf_op jit(solution)/shard_map/while/body/eval_jaxpr/cond/branch_1_fun/all_to_all | solution.py:247
  107.1 9.9 %experts.1 = bf16[256,3072]{1,0:T(8,128)(2,1)S(1)} custom-call(bf16[256,3072]{1,0:T(8,128)(2,1)S(1)} %bitcast.27, bf16[2,2048,768]{2,1,0:T(8,128)(2,1)} %bitcast.30, bf16[2,2048,768]{2,1,0:T(8,128)(2,1)} %bitcast.31, bf16[2,768,2048]{2,1,0:T(8,128)(2,1)} %bitcast.32), custom_call_target="tpu_custom_call" | custom-call | tf_op jit(solution)/shard_map/while/body/eval_jaxpr/cond/branch_1_fun/experts/pallas_call | solution.py:266
  117.1 24.8 %all_to_all.17 = bf16[16,16,3072]{2,1,0:T(8,128)(2,1)S(1)} all-to-all(bf16[16,16,3072]{2,1,0:T(8,128)(2,1)S(1)} %bitcast.28), channel_id=1, replica_groups=mesh['pipe'=4,'exp'=16,'pair'=2] {'exp'}, dimensions={0} | all-to-all | bytes 3145728 | tf_op jit(solution)/shard_map/while/body/eval_jaxpr/cond/branch_1_fun/all_to_all | solution.py:247
  143.5 1.9 collective-permute-start
  145.4 1.9 collective-permute-start.1
  148.7 4.4 collective-permute-done.1
  153.2 64.8 %conditional.2 = (bf16[64,2048]{1,0:T(8,128)(2,1)S(1)}) conditional(s32[]{:T(128)} %convert_element_type.30, bf16[64,2048]{1,0:T(8,128)(2,1)S(1)} %copy.20, (s32[1,4,32,8]{3,2,1,0:T(8,128)S(1)}, s32[3]{0:T(128)S(1)}, bf16[4,32,2048]{2,1,0:T(8,128)(2,1)}, bf16[4,32,2048]{2,1,0:T(8,128)(2,1)S(1)}, bf16[64,2048]{1,0:T(8,128)(2,1)S(1)}, ...), branch_computations={%region_1.1_spmd, %region_2.2_spmd} | conditional | bytes 6291464 | solution.py:271
  153.2 2.3 dispatch.1
  155.6 26.3 %all_to_all.16 = bf16[16,16,3072]{2,1,0:T(8,128)(2,1)S(1)} all-to-all(bf16[16,16,3072]{2,1,0:T(8,128)(2,1)S(1)} %bitcast.29), channel_id=1, replica_groups=mesh['pipe'=4,'exp'=16,'pair'=2] {'exp'}, dimensions={0} | all-to-all | bytes 3145728 | tf_op jit(solution)/shard_map/while/body/eval_jaxpr/cond/branch_1_fun/all_to_all | solution.py:247
  181.8 9.9 %experts.1 = bf16[256,3072]{1,0:T(8,128)(2,1)S(1)} custom-call(bf16[256,3072]{1,0:T(8,128)(2,1)S(1)} %bitcast.27, bf16[2,2048,768]{2,1,0:T(8,128)(2,1)} %bitcast.30, bf16[2,2048,768]{2,1,0:T(8,128)(2,1)} %bitcast.31, bf16[2,768,2048]{2,1,0:T(8,128)(2,1)} %bitcast.32), custom_call_target="tpu_custom_call" | custom-call | tf_op jit(solution)/shard_map/while/body/eval_jaxpr/cond/branch_1_fun/experts/pallas_call | solution.py:266
  191.8 24.7 %all_to_all.17 = bf16[16,16,3072]{2,1,0:T(8,128)(2,1)S(1)} all-to-all(bf16[16,16,3072]{2,1,0:T(8,128)(2,1)S(1)} %bitcast.28), channel_id=1, replica_groups=mesh['pipe'=4,'exp'=16,'pair'=2] {'exp'}, dimensions={0} | all-to-all | bytes 3145728 | tf_op jit(solution)/shard_map/while/body/eval_jaxpr/cond/branch_1_fun/all_to_all | solution.py:247
  218.1 1.9 collective-permute-start
  220.0 1.9 collective-permute-start.1
  223.3 4.4 collective-permute-done.1
  227.8 65.2 %conditional.2 = (bf16[64,2048]{1,0:T(8,128)(2,1)S(1)}) conditional(s32[]{:T(128)} %convert_element_type.30, bf16[64,2048]{1,0:T(8,128)(2,1)S(1)} %copy.20, (s32[1,4,32,8]{3,2,1,0:T(8,128)S(1)}, s32[3]{0:T(128)S(1)}, bf16[4,32,2048]{2,1,0:T(8,128)(2,1)}, bf16[4,32,2048]{2,1,0:T(8,128)(2,1)S(1)}, bf16[64,2048]{1,0:T(8,128)(2,1)S(1)}, ...), branch_computations={%region_1.1_spmd, %region_2.2_spmd} | conditional | bytes 6291464 | solution.py:271
  227.8 2.3 dispatch.1
  230.2 26.4 %all_to_all.16 = bf16[16,16,3072]{2,1,0:T(8,128)(2,1)S(1)} all-to-all(bf16[16,16,3072]{2,1,0:T(8,128)(2,1)S(1)} %bitcast.29), channel_id=1, replica_groups=mesh['pipe'=4,'exp'=16,'pair'=2] {'exp'}, dimensions={0} | all-to-all | bytes 3145728 | tf_op jit(solution)/shard_map/while/body/eval_jaxpr/cond/branch_1_fun/all_to_all | solution.py:247
  256.5 9.9 %experts.1 = bf16[256,3072]{1,0:T(8,128)(2,1)S(1)} custom-call(bf16[256,3072]{1,0:T(8,128)(2,1)S(1)} %bitcast.27, bf16[2,2048,768]{2,1,0:T(8,128)(2,1)} %bitcast.30, bf16[2,2048,768]{2,1,0:T(8,128)(2,1)} %bitcast.31, bf16[2,768,2048]{2,1,0:T(8,128)(2,1)} %bitcast.32), custom_call_target="tpu_custom_call" | custom-call | tf_op jit(solution)/shard_map/while/body/eval_jaxpr/cond/branch_1_fun/experts/pallas_call | solution.py:266
  266.5 24.9 %all_to_all.17 = bf16[16,16,3072]{2,1,0:T(8,128)(2,1)S(1)} all-to-all(bf16[16,16,3072]{2,1,0:T(8,128)(2,1)S(1)} %bitcast.28), channel_id=1, replica_groups=mesh['pipe'=4,'exp'=16,'pair'=2] {'exp'}, dimensions={0} | all-to-all | bytes 3145728 | tf_op jit(solution)/shard_map/while/body/eval_jaxpr/cond/branch_1_fun/all_to_all | solution.py:247
  291.4 1.6 combine.1
  293.0 1.9 collective-permute-start
  294.9 1.9 collective-permute-start.1
  298.2 4.4 collective-permute-done.1
  302.7 49.5 %conditional.2 = (bf16[64,2048]{1,0:T(8,128)(2,1)S(1)}) conditional(s32[]{:T(128)} %convert_element_type.30, bf16[64,2048]{1,0:T(8,128)(2,1)S(1)} %copy.20, (s32[1,4,32,8]{3,2,1,0:T(8,128)S(1)}, s32[3]{0:T(128)S(1)}, bf16[4,32,2048]{2,1,0:T(8,128)(2,1)}, bf16[4,32,2048]{2,1,0:T(8,128)(2,1)S(1)}, bf16[64,2048]{1,0:T(8,128)(2,1)S(1)}, ...), branch_computations={%region_1.1_spmd, %region_2.2_spmd} | conditional | bytes 6291464 | solution.py:271
  302.7 2.3 dispatch.1
  305.1 18.1 %all_to_all.16 = bf16[16,16,3072]{2,1,0:T(8,128)(2,1)S(1)} all-to-all(bf16[16,16,3072]{2,1,0:T(8,128)(2,1)S(1)} %bitcast.29), channel_id=1, replica_groups=mesh['pipe'=4,'exp'=16,'pair'=2] {'exp'}, dimensions={0} | all-to-all | bytes 3145728 | tf_op jit(solution)/shard_map/while/body/eval_jaxpr/cond/branch_1_fun/all_to_all | solution.py:247
  323.2 9.9 %experts.1 = bf16[256,3072]{1,0:T(8,128)(2,1)S(1)} custom-call(bf16[256,3072]{1,0:T(8,128)(2,1)S(1)} %bitcast.27, bf16[2,2048,768]{2,1,0:T(8,128)(2,1)} %bitcast.30, bf16[2,2048,768]{2,1,0:T(8,128)(2,1)} %bitcast.31, bf16[2,768,2048]{2,1,0:T(8,128)(2,1)} %bitcast.32), custom_call_target="tpu_custom_call" | custom-call | tf_op jit(solution)/shard_map/while/body/eval_jaxpr/cond/branch_1_fun/experts/pallas_call | solution.py:266
  333.1 17.5 %all_to_all.17 = bf16[16,16,3072]{2,1,0:T(8,128)(2,1)S(1)} all-to-all(bf16[16,16,3072]{2,1,0:T(8,128)(2,1)S(1)} %bitcast.28), channel_id=1, replica_groups=mesh['pipe'=4,'exp'=16,'pair'=2] {'exp'}, dimensions={0} | all-to-all | bytes 3145728 | tf_op jit(solution)/shard_map/while/body/eval_jaxpr/cond/branch_1_fun/all_to_all | solution.py:247
  352.2 7.2 %collective-permute-start = (bf16[64,2048]{1,0:T(8,128)(2,1)S(1)}, bf16[64,2048]{1,0:T(8,128)(2,1)S(1)}, u32[]{:S(2)}, u32[]{:S(2)}) collective-permute-start(bf16[64,2048]{1,0:T(8,128)(2,1)S(1)} %get-tuple-element.604), channel_id=1, source_target_pairs={{0,32},{1,33},{32,64},{33,65},{64,96},{65,97},{2,34},{3,35},{34,66... | collective-permute-start | bytes 786440 | tf_op jit(solution)/shard_map/while/body/eval_jaxpr/ppermute | solution.py:273
  359.4 2.3 collective-permute-start.1
  362.7 4.4 collective-permute-done.1
  367.2 65.5 %collective-permute-start = (bf16[64,2048]{1,0:T(8,128)(2,1)S(1)}, bf16[64,2048]{1,0:T(8,128)(2,1)S(1)}, u32[]{:S(2)}, u32[]{:S(2)}) collective-permute-start(bf16[64,2048]{1,0:T(8,128)(2,1)S(1)} %get-tuple-element.604), channel_id=1, source_target_pairs={{0,32},{1,33},{32,64},{33,65},{64,96},{65,97},{2,34},{3,35},{34,66... | collective-permute-start | bytes 786440 | tf_op jit(solution)/shard_map/while/body/eval_jaxpr/ppermute | solution.py:273
  432.7 1.9 collective-permute-start.1
  434.6 3.5 collective-permute-done
  438.2 2.2 collective-permute-done.1
  440.5 4.3 collective-permute-start
  444.8 48.1 %collective-permute-start.1 = (bf16[64,2048]{1,0:T(8,128)(2,1)S(1)}, bf16[64,2048]{1,0:T(8,128)(2,1)S(1)}, u32[]{:S(2)}, u32[]{:S(2)}) collective-permute-start(bf16[64,2048]{1,0:T(8,128)(2,1)S(1)} %get-tuple-element.604), channel_id=1, source_target_pairs={{0,33},{1,32},{32,65},{33,64},{64,97},{65,96},{2,35},{3,34},{34,67... | collective-permute-start | bytes 786440 | tf_op jit(solution)/shard_map/while/body/eval_jaxpr/ppermute | solution.py:274
  493.0 3.3 collective-permute-done.1
  496.4 8.0 %collective-permute-done.5 = bf16[4,32,2048]{2,1,0:T(8,128)(2,1)S(1)} collective-permute-done((bf16[4,32,2048]{2,1,0:T(8,128)(2,1)S(1)}, bf16[4,32,2048]{2,1,0:T(8,128)(2,1)S(1)}, u32[]{:S(2)}, u32[]{:S(2)}) %collective-permute-start.5) | collective-permute-done | bytes 524320 | tf_op jit(solution)/shard_map/ppermute | solution.py:283
  (44 shorter events, 14.7 us)
Async XLA Ops:
  0.0 8.6 %collective-permute-start.2 = (bf16[4,32,2048]{2,1,0:T(8,128)(2,1)}, bf16[4,32,2048]{2,1,0:T(8,128)(2,1)S(1)}, u32[]{:S(2)}, u32[]{:S(2)}) collective-permute-start(bf16[4,32,2048]{2,1,0:T(8,128)(2,1)} %param.11), channel_id=1, source_target_pairs={{0,1},{1,0},{2,3},{3,2},{4,5},{5,4},{6,7},{7,6},{8,9},{9,8},{10,11... | collective-permute-start | bytes 1572872 | tf_op jit(solution)/shard_map/ppermute | solution.py:251
  1.5 3.8 collective-permute-start.3
  4.5 4.2 collective-permute-start.4
  8.8 64.8 %collective-permute-start = (bf16[64,2048]{1,0:T(8,128)(2,1)S(1)}, bf16[64,2048]{1,0:T(8,128)(2,1)S(1)}, u32[]{:S(2)}, u32[]{:S(2)}) collective-permute-start(bf16[64,2048]{1,0:T(8,128)(2,1)S(1)} %get-tuple-element.604), channel_id=1, source_target_pairs={{0,32},{1,33},{32,64},{33,65},{64,96},{65,97},{2,34},{3,35},{34,66... | collective-permute-start | bytes 786440 | tf_op jit(solution)/shard_map/while/body/eval_jaxpr/ppermute | solution.py:273
  14.3 64.1 %collective-permute-start.1 = (bf16[64,2048]{1,0:T(8,128)(2,1)S(1)}, bf16[64,2048]{1,0:T(8,128)(2,1)S(1)}, u32[]{:S(2)}, u32[]{:S(2)}) collective-permute-start(bf16[64,2048]{1,0:T(8,128)(2,1)S(1)} %get-tuple-element.604), channel_id=1, source_target_pairs={{0,33},{1,32},{32,65},{33,64},{64,97},{65,96},{2,35},{3,34},{34,67... | collective-permute-start | bytes 786440 | tf_op jit(solution)/shard_map/while/body/eval_jaxpr/ppermute | solution.py:274
  143.5 5.2 %collective-permute-start = (bf16[64,2048]{1,0:T(8,128)(2,1)S(1)}, bf16[64,2048]{1,0:T(8,128)(2,1)S(1)}, u32[]{:S(2)}, u32[]{:S(2)}) collective-permute-start(bf16[64,2048]{1,0:T(8,128)(2,1)S(1)} %get-tuple-element.604), channel_id=1, source_target_pairs={{0,32},{1,33},{32,64},{33,65},{64,96},{65,97},{2,34},{3,35},{34,66... | collective-permute-start | bytes 786440 | tf_op jit(solution)/shard_map/while/body/eval_jaxpr/ppermute | solution.py:273
  145.4 7.7 %collective-permute-start.1 = (bf16[64,2048]{1,0:T(8,128)(2,1)S(1)}, bf16[64,2048]{1,0:T(8,128)(2,1)S(1)}, u32[]{:S(2)}, u32[]{:S(2)}) collective-permute-start(bf16[64,2048]{1,0:T(8,128)(2,1)S(1)} %get-tuple-element.604), channel_id=1, source_target_pairs={{0,33},{1,32},{32,65},{33,64},{64,97},{65,96},{2,35},{3,34},{34,67... | collective-permute-start | bytes 786440 | tf_op jit(solution)/shard_map/while/body/eval_jaxpr/ppermute | solution.py:274
  218.1 5.2 %collective-permute-start = (bf16[64,2048]{1,0:T(8,128)(2,1)S(1)}, bf16[64,2048]{1,0:T(8,128)(2,1)S(1)}, u32[]{:S(2)}, u32[]{:S(2)}) collective-permute-start(bf16[64,2048]{1,0:T(8,128)(2,1)S(1)} %get-tuple-element.604), channel_id=1, source_target_pairs={{0,32},{1,33},{32,64},{33,65},{64,96},{65,97},{2,34},{3,35},{34,66... | collective-permute-start | bytes 786440 | tf_op jit(solution)/shard_map/while/body/eval_jaxpr/ppermute | solution.py:273
  220.0 7.7 %collective-permute-start.1 = (bf16[64,2048]{1,0:T(8,128)(2,1)S(1)}, bf16[64,2048]{1,0:T(8,128)(2,1)S(1)}, u32[]{:S(2)}, u32[]{:S(2)}) collective-permute-start(bf16[64,2048]{1,0:T(8,128)(2,1)S(1)} %get-tuple-element.604), channel_id=1, source_target_pairs={{0,33},{1,32},{32,65},{33,64},{64,97},{65,96},{2,35},{3,34},{34,67... | collective-permute-start | bytes 786440 | tf_op jit(solution)/shard_map/while/body/eval_jaxpr/ppermute | solution.py:274
  293.0 5.2 %collective-permute-start = (bf16[64,2048]{1,0:T(8,128)(2,1)S(1)}, bf16[64,2048]{1,0:T(8,128)(2,1)S(1)}, u32[]{:S(2)}, u32[]{:S(2)}) collective-permute-start(bf16[64,2048]{1,0:T(8,128)(2,1)S(1)} %get-tuple-element.604), channel_id=1, source_target_pairs={{0,32},{1,33},{32,64},{33,65},{64,96},{65,97},{2,34},{3,35},{34,66... | collective-permute-start | bytes 786440 | tf_op jit(solution)/shard_map/while/body/eval_jaxpr/ppermute | solution.py:273
  294.9 7.7 %collective-permute-start.1 = (bf16[64,2048]{1,0:T(8,128)(2,1)S(1)}, bf16[64,2048]{1,0:T(8,128)(2,1)S(1)}, u32[]{:S(2)}, u32[]{:S(2)}) collective-permute-start(bf16[64,2048]{1,0:T(8,128)(2,1)S(1)} %get-tuple-element.604), channel_id=1, source_target_pairs={{0,33},{1,32},{32,65},{33,64},{64,97},{65,96},{2,35},{3,34},{34,67... | collective-permute-start | bytes 786440 | tf_op jit(solution)/shard_map/while/body/eval_jaxpr/ppermute | solution.py:274
  352.2 10.5 %collective-permute-start = (bf16[64,2048]{1,0:T(8,128)(2,1)S(1)}, bf16[64,2048]{1,0:T(8,128)(2,1)S(1)}, u32[]{:S(2)}, u32[]{:S(2)}) collective-permute-start(bf16[64,2048]{1,0:T(8,128)(2,1)S(1)} %get-tuple-element.604), channel_id=1, source_target_pairs={{0,32},{1,33},{32,64},{33,65},{64,96},{65,97},{2,34},{3,35},{34,66... | collective-permute-start | bytes 786440 | tf_op jit(solution)/shard_map/while/body/eval_jaxpr/ppermute | solution.py:273
  359.4 7.7 %collective-permute-start.1 = (bf16[64,2048]{1,0:T(8,128)(2,1)S(1)}, bf16[64,2048]{1,0:T(8,128)(2,1)S(1)}, u32[]{:S(2)}, u32[]{:S(2)}) collective-permute-start(bf16[64,2048]{1,0:T(8,128)(2,1)S(1)} %get-tuple-element.604), channel_id=1, source_target_pairs={{0,33},{1,32},{32,65},{33,64},{64,97},{65,96},{2,35},{3,34},{34,67... | collective-permute-start | bytes 786440 | tf_op jit(solution)/shard_map/while/body/eval_jaxpr/ppermute | solution.py:274
  367.2 71.0 %collective-permute-start = (bf16[64,2048]{1,0:T(8,128)(2,1)S(1)}, bf16[64,2048]{1,0:T(8,128)(2,1)S(1)}, u32[]{:S(2)}, u32[]{:S(2)}) collective-permute-start(bf16[64,2048]{1,0:T(8,128)(2,1)S(1)} %get-tuple-element.604), channel_id=1, source_target_pairs={{0,32},{1,33},{32,64},{33,65},{64,96},{65,97},{2,34},{3,35},{34,66... | collective-permute-start | bytes 786440 | tf_op jit(solution)/shard_map/while/body/eval_jaxpr/ppermute | solution.py:273
  432.7 7.7 %collective-permute-start.1 = (bf16[64,2048]{1,0:T(8,128)(2,1)S(1)}, bf16[64,2048]{1,0:T(8,128)(2,1)S(1)}, u32[]{:S(2)}, u32[]{:S(2)}) collective-permute-start(bf16[64,2048]{1,0:T(8,128)(2,1)S(1)} %get-tuple-element.604), channel_id=1, source_target_pairs={{0,33},{1,32},{32,65},{33,64},{64,97},{65,96},{2,35},{3,34},{34,67... | collective-permute-start | bytes 786440 | tf_op jit(solution)/shard_map/while/body/eval_jaxpr/ppermute | solution.py:274
  440.5 52.5 %collective-permute-start = (bf16[64,2048]{1,0:T(8,128)(2,1)S(1)}, bf16[64,2048]{1,0:T(8,128)(2,1)S(1)}, u32[]{:S(2)}, u32[]{:S(2)}) collective-permute-start(bf16[64,2048]{1,0:T(8,128)(2,1)S(1)} %get-tuple-element.604), channel_id=1, source_target_pairs={{0,32},{1,33},{32,64},{33,65},{64,96},{65,97},{2,34},{3,35},{34,66... | collective-permute-start | bytes 786440 | tf_op jit(solution)/shard_map/while/body/eval_jaxpr/ppermute | solution.py:273
  444.8 51.4 %collective-permute-start.1 = (bf16[64,2048]{1,0:T(8,128)(2,1)S(1)}, bf16[64,2048]{1,0:T(8,128)(2,1)S(1)}, u32[]{:S(2)}, u32[]{:S(2)}) collective-permute-start(bf16[64,2048]{1,0:T(8,128)(2,1)S(1)} %get-tuple-element.604), channel_id=1, source_target_pairs={{0,33},{1,32},{32,65},{33,64},{64,97},{65,96},{2,35},{3,34},{34,67... | collective-permute-start | bytes 786440 | tf_op jit(solution)/shard_map/while/body/eval_jaxpr/ppermute | solution.py:274
  496.3 8.1 %collective-permute-start.5 = (bf16[4,32,2048]{2,1,0:T(8,128)(2,1)S(1)}, bf16[4,32,2048]{2,1,0:T(8,128)(2,1)S(1)}, u32[]{:S(2)}, u32[]{:S(2)}) collective-permute-start(bf16[4,32,2048]{2,1,0:T(8,128)(2,1)S(1)} %constant_dynamic-slice_fusion), channel_id=1, source_target_pairs={{0,1},{1,0},{2,3},{3,2},{4,5},{5,4},{6,7},{7,6},{8,9},{9,8},{10,11... | collective-permute-start | bytes 1572872 | tf_op jit(solution)/shard_map/ppermute | solution.py:283

commit v3 on v2

--- a/solution.py
+++ b/solution.py
@@ -8,6 +8,7 @@
 from jax.sharding import PartitionSpec as P
 
 EPS = 1e-06
+STAGGER_NS = 8000
 F32 = jnp.float32
 BF16 = jnp.bfloat16
 GROUP = ("exp", "pair")
@@ -62,6 +63,11 @@
     where_ref, hidden_ref, other_ref, same_ref, cross_ref, routes_ref, routes_other_ref, gain_ref, out_ref, state_ref, *, experts
 ):
     index, section, side = where_ref[0], where_ref[1], where_ref[2]
+
+    @pl.when(where_ref[3] == 1)
+    def _():
+        pl.delay(STAGGER_NS)
+
     rows = out_ref.shape[0]
     tokens = hidden_ref.shape[1]
     width = state_ref.shape[1]
@@ -254,10 +260,13 @@
     onward = [(2 * s + y, 2 * s + 2 + y) for s in range(stages - 1) for y in range(2)]
     across = [(2 * s + y, 2 * s + 3 - y) for s in range(stages - 1) for y in range(2)]
 
+    steps = micro + stages - 1
+
     def advance(step, carry):
         same, cross, made = carry
         index = jnp.clip(step - section, 0, micro - 1)
-        where = jnp.stack([index, section, side]).astype(jnp.int32)
+        late = (section == 1) & (index < micro - 1)
+        where = jnp.stack([index, section, side, late.astype(jnp.int32)])
 
         def layer():
             packets, state = dispatch(
@@ -270,11 +279,13 @@
 
         part = lax.cond((step >= section) & (step < section + micro), layer, lambda: same)
         made = lax.dynamic_update_index_in_dim(made, part, step, 0)
-        same = lax.ppermute(part, stage_pair, onward)
-        cross = lax.ppermute(part, stage_pair, across)
+
+        def relay():
+            return lax.ppermute(part, stage_pair, onward), lax.ppermute(part, stage_pair, across)
+
+        same, cross = lax.cond(step < steps - 1, relay, lambda: (same, cross))
         return same, cross, made
 
-    steps = micro + stages - 1
     blank = jnp.zeros((2 * tokens, width), BF16)
     start = (blank, blank, jnp.zeros((steps, 2 * tokens, width), BF16))
     same, cross, made = lax.fori_loop(0, steps, advance, start)

time: 510 us -> 480 us (0.941)
  the two profiles are of different devices: /device:TPU:1 before, /device:TPU:17 now
where the time goes in v3:
time: 480 us; the launch traced here: 479 us
  waiting for transfers between devices  248 us (52%)
  blocking collectives  149 us (31%)
  Pallas kernels  56.1 us (12%)
  starting transfers between devices  17.9 us (4%)
  local copies, waits for them, and re-layouts  6.09 us (1%)
    ppermute x6, waiting for transfers between devices, relay(): lax.ppermute(part, stage_pair, onward)  202 us
    all_to_all x8, blocking collectives, exchange(): lax.all_to_all(packets, 'exp', split_axis=0, concat_axis=0, tiled=True)  149 us
    pallas_call x4, Pallas kernels, layer(): produced = experts(exchange(packets), w_gate[0], w_up[0], w_down[0])  39.8 us
    ppermute x6, waiting for transfers between devices, relay(): lax.ppermute(part, stage_pair, across)  35.5 us
    pallas_call x4, Pallas kernels, layer(): dispatch(where, hidden_in, hidden_other, same, cross, routes[0], routes_o...  9.97 us
  transfers between devices with their start and end apart: 16, of which 15 were waited for; matrix products, arithmetic and copies ran while one was open for 0% of the time, Pallas kernels for 0%

profile of v3, /device:TPU:17, one launch (start us, length us, event | category | flops | bytes accessed | tf_op | source)
XLA Modules:
  0.0 479.0 jit_solution(7022589276460432012)
XLA Ops:
  4.7 1.9 collective-permute-done.4
  8.0 461.9 %while.21 = (s32[]{:T(128)}, bf16[64,2048]{1,0:T(8,128)(2,1)}, bf16[64,2048]{1,0:T(8,128)(2,1)}, bf16[7,64,2048]{2,1,0:T(8,128)(2,1)S(1)}, s32[]{:T(128)}, /*ind...) while((s32[]{:T(128)}, bf16[64,2048]{1,0:T(8,128)(2,1)}, ...), condition=%wide.region_5.6_spmd, body=%wide.region_0.5_spmd.sunk | while | flops 26 | bytes 8913454 | solution.py:291
  9.0 10.8 %conditional.5 = ((bf16[64,2048]{1,0:T(8,128)(2,1)}, bf16[64,2048]{1,0:T(8,128)(2,1)})) conditional(s32[]{:T(128)} %convert_element_type.45, (bf16[64,2048]{1,0:T(8,128)(2,1)}, bf16[64,2048]{1,0:T(8,128)(2,1)}) %tuple.53, bf16[64,2048]{1,0:T(8,128)(2,1)S(1)} %get-tuple-element.637), branch_computations={%region_3.3_spmd, %region_4.4_spmd} | conditional | bytes 2097256 | solution.py:286
  9.0 1.3 collective-permute-start
  11.6 2.6 collective-permute-done
  14.2 5.6 %collective-permute-done.1 = bf16[64,2048]{1,0:T(8,128)(2,1)} collective-permute-done((bf16[64,2048]{1,0:T(8,128)(2,1)S(1)}, bf16[64,2048]{1,0:T(8,128)(2,1)}, u32[]{:S(2)}, u32[]{:S(2)}) %collective-permute-start.1) | collective-permute-done | bytes 262176 | tf_op jit(solution)/shard_map/while/body/eval_jaxpr/cond/branch_1_fun/ppermute | solution.py:284
  20.8 11.8 %conditional.5 = ((bf16[64,2048]{1,0:T(8,128)(2,1)}, bf16[64,2048]{1,0:T(8,128)(2,1)})) conditional(s32[]{:T(128)} %convert_element_type.45, (bf16[64,2048]{1,0:T(8,128)(2,1)}, bf16[64,2048]{1,0:T(8,128)(2,1)}) %tuple.53, bf16[64,2048]{1,0:T(8,128)(2,1)S(1)} %get-tuple-element.637), branch_computations={%region_3.3_spmd, %region_4.4_spmd} | conditional | bytes 2097256 | solution.py:286
  23.4 3.9 collective-permute-done
  27.4 5.3 %collective-permute-done.1 = bf16[64,2048]{1,0:T(8,128)(2,1)} collective-permute-done((bf16[64,2048]{1,0:T(8,128)(2,1)S(1)}, bf16[64,2048]{1,0:T(8,128)(2,1)}, u32[]{:S(2)}, u32[]{:S(2)}) %collective-permute-start.1) | collective-permute-done | bytes 262176 | tf_op jit(solution)/shard_map/while/body/eval_jaxpr/cond/branch_1_fun/ppermute | solution.py:284
  33.7 176.2 %conditional.5 = ((bf16[64,2048]{1,0:T(8,128)(2,1)}, bf16[64,2048]{1,0:T(8,128)(2,1)})) conditional(s32[]{:T(128)} %convert_element_type.45, (bf16[64,2048]{1,0:T(8,128)(2,1)}, bf16[64,2048]{1,0:T(8,128)(2,1)}) %tuple.53, bf16[64,2048]{1,0:T(8,128)(2,1)S(1)} %get-tuple-element.637), branch_computations={%region_3.3_spmd, %region_4.4_spmd} | conditional | bytes 2097256 | solution.py:286
  36.3 167.6 %collective-permute-done = bf16[64,2048]{1,0:T(8,128)(2,1)} collective-permute-done((bf16[64,2048]{1,0:T(8,128)(2,1)S(1)}, bf16[64,2048]{1,0:T(8,128)(2,1)}, u32[]{:S(2)}, u32[]{:S(2)}) %collective-permute-start) | collective-permute-done | bytes 262176 | tf_op jit(solution)/shard_map/while/body/eval_jaxpr/cond/branch_1_fun/ppermute | solution.py:284
  203.9 6.0 %collective-permute-done.1 = bf16[64,2048]{1,0:T(8,128)(2,1)} collective-permute-done((bf16[64,2048]{1,0:T(8,128)(2,1)S(1)}, bf16[64,2048]{1,0:T(8,128)(2,1)}, u32[]{:S(2)}, u32[]{:S(2)}) %collective-permute-start.1) | collective-permute-done | bytes 262176 | tf_op jit(solution)/shard_map/while/body/eval_jaxpr/cond/branch_1_fun/ppermute | solution.py:284
  210.0 49.4 %conditional.4 = (bf16[64,2048]{1,0:T(8,128)(2,1)S(1)}) conditional(s32[]{:T(128)} %convert_element_type.46, bf16[64,2048]{1,0:T(8,128)(2,1)} %get-tuple-element.594, (s32[1,4,32,8]{3,2,1,0:T(8,128)S(1)}, s32[4]{0:T(128)S(1)}, bf16[4,32,2048]{2,1,0:T(8,128)(2,1)}, bf16[4,32,2048]{2,1,0:T(8,128)(2,1)S(1)}, bf16[64,2048]{1,0:T(8,128)(2,1)}, ...), branch_computations={%region_1.1_spmd, %region_2.2_spmd} | conditional | bytes 6291464 | solution.py:280
  210.0 2.5 dispatch.1
  212.5 17.8 %all_to_all.16 = bf16[16,16,3072]{2,1,0:T(8,128)(2,1)S(1)} all-to-all(bf16[16,16,3072]{2,1,0:T(8,128)(2,1)S(1)} %bitcast.32), channel_id=1, replica_groups=mesh['pipe'=4,'exp'=16,'pair'=2] {'exp'}, dimensions={0} | all-to-all | bytes 3145728 | tf_op jit(solution)/shard_map/while/body/eval_jaxpr/cond/branch_1_fun/all_to_all | solution.py:253
  230.2 9.9 %experts.1 = bf16[256,3072]{1,0:T(8,128)(2,1)S(1)} custom-call(bf16[256,3072]{1,0:T(8,128)(2,1)S(1)} %bitcast.30, bf16[2,2048,768]{2,1,0:T(8,128)(2,1)} %bitcast.33, bf16[2,2048,768]{2,1,0:T(8,128)(2,1)} %bitcast.34, bf16[2,768,2048]{2,1,0:T(8,128)(2,1)} %bitcast.35), custom_call_target="tpu_custom_call" | custom-call | tf_op jit(solution)/shard_map/while/body/eval_jaxpr/cond/branch_1_fun/experts/pallas_call | solution.py:275
  240.2 17.6 %all_to_all.17 = bf16[16,16,3072]{2,1,0:T(8,128)(2,1)S(1)} all-to-all(bf16[16,16,3072]{2,1,0:T(8,128)(2,1)S(1)} %bitcast.31), channel_id=1, replica_groups=mesh['pipe'=4,'exp'=16,'pair'=2] {'exp'}, dimensions={0} | all-to-all | bytes 3145728 | tf_op jit(solution)/shard_map/while/body/eval_jaxpr/cond/branch_1_fun/all_to_all | solution.py:253
  257.8 1.6 combine.1
  259.4 19.8 %conditional.5 = ((bf16[64,2048]{1,0:T(8,128)(2,1)}, bf16[64,2048]{1,0:T(8,128)(2,1)})) conditional(s32[]{:T(128)} %convert_element_type.45, (bf16[64,2048]{1,0:T(8,128)(2,1)}, bf16[64,2048]{1,0:T(8,128)(2,1)}) %tuple.53, bf16[64,2048]{1,0:T(8,128)(2,1)S(1)} %get-tuple-element.637), branch_computations={%region_3.3_spmd, %region_4.4_spmd} | conditional | bytes 2097256 | solution.py:286
  259.4 1.3 collective-permute-start
  260.7 1.3 collective-permute-start.1
  262.0 10.7 %collective-permute-done = bf16[64,2048]{1,0:T(8,128)(2,1)} collective-permute-done((bf16[64,2048]{1,0:T(8,128)(2,1)S(1)}, bf16[64,2048]{1,0:T(8,128)(2,1)}, u32[]{:S(2)}, u32[]{:S(2)}) %collective-permute-start) | collective-permute-done | bytes 262176 | tf_op jit(solution)/shard_map/while/body/eval_jaxpr/cond/branch_1_fun/ppermute | solution.py:284
  272.7 6.5 %collective-permute-done.1 = bf16[64,2048]{1,0:T(8,128)(2,1)} collective-permute-done((bf16[64,2048]{1,0:T(8,128)(2,1)S(1)}, bf16[64,2048]{1,0:T(8,128)(2,1)}, u32[]{:S(2)}, u32[]{:S(2)}) %collective-permute-start.1) | collective-permute-done | bytes 262176 | tf_op jit(solution)/shard_map/while/body/eval_jaxpr/cond/branch_1_fun/ppermute | solution.py:284
  279.3 49.4 %conditional.4 = (bf16[64,2048]{1,0:T(8,128)(2,1)S(1)}) conditional(s32[]{:T(128)} %convert_element_type.46, bf16[64,2048]{1,0:T(8,128)(2,1)} %get-tuple-element.594, (s32[1,4,32,8]{3,2,1,0:T(8,128)S(1)}, s32[4]{0:T(128)S(1)}, bf16[4,32,2048]{2,1,0:T(8,128)(2,1)}, bf16[4,32,2048]{2,1,0:T(8,128)(2,1)S(1)}, bf16[64,2048]{1,0:T(8,128)(2,1)}, ...), branch_computations={%region_1.1_spmd, %region_2.2_spmd} | conditional | bytes 6291464 | solution.py:280
  279.3 2.5 dispatch.1
  281.8 17.7 %all_to_all.16 = bf16[16,16,3072]{2,1,0:T(8,128)(2,1)S(1)} all-to-all(bf16[16,16,3072]{2,1,0:T(8,128)(2,1)S(1)} %bitcast.32), channel_id=1, replica_groups=mesh['pipe'=4,'exp'=16,'pair'=2] {'exp'}, dimensions={0} | all-to-all | bytes 3145728 | tf_op jit(solution)/shard_map/while/body/eval_jaxpr/cond/branch_1_fun/all_to_all | solution.py:253
  299.5 9.9 %experts.1 = bf16[256,3072]{1,0:T(8,128)(2,1)S(1)} custom-call(bf16[256,3072]{1,0:T(8,128)(2,1)S(1)} %bitcast.30, bf16[2,2048,768]{2,1,0:T(8,128)(2,1)} %bitcast.33, bf16[2,2048,768]{2,1,0:T(8,128)(2,1)} %bitcast.34, bf16[2,768,2048]{2,1,0:T(8,128)(2,1)} %bitcast.35), custom_call_target="tpu_custom_call" | custom-call | tf_op jit(solution)/shard_map/while/body/eval_jaxpr/cond/branch_1_fun/experts/pallas_call | solution.py:275
  309.4 17.7 %all_to_all.17 = bf16[16,16,3072]{2,1,0:T(8,128)(2,1)S(1)} all-to-all(bf16[16,16,3072]{2,1,0:T(8,128)(2,1)S(1)} %bitcast.31), channel_id=1, replica_groups=mesh['pipe'=4,'exp'=16,'pair'=2] {'exp'}, dimensions={0} | all-to-all | bytes 3145728 | tf_op jit(solution)/shard_map/while/body/eval_jaxpr/cond/branch_1_fun/all_to_all | solution.py:253
  327.1 1.6 combine.1
  328.8 19.2 %conditional.5 = ((bf16[64,2048]{1,0:T(8,128)(2,1)}, bf16[64,2048]{1,0:T(8,128)(2,1)})) conditional(s32[]{:T(128)} %convert_element_type.45, (bf16[64,2048]{1,0:T(8,128)(2,1)}, bf16[64,2048]{1,0:T(8,128)(2,1)}) %tuple.53, bf16[64,2048]{1,0:T(8,128)(2,1)S(1)} %get-tuple-element.637), branch_computations={%region_3.3_spmd, %region_4.4_spmd} | conditional | bytes 2097256 | solution.py:286
  331.4 11.1 %collective-permute-done = bf16[64,2048]{1,0:T(8,128)(2,1)} collective-permute-done((bf16[64,2048]{1,0:T(8,128)(2,1)S(1)}, bf16[64,2048]{1,0:T(8,128)(2,1)}, u32[]{:S(2)}, u32[]{:S(2)}) %collective-permute-start) | collective-permute-done | bytes 262176 | tf_op jit(solution)/shard_map/while/body/eval_jaxpr/cond/branch_1_fun/ppermute | solution.py:284
  342.4 5.5 %collective-permute-done.1 = bf16[64,2048]{1,0:T(8,128)(2,1)} collective-permute-done((bf16[64,2048]{1,0:T(8,128)(2,1)S(1)}, bf16[64,2048]{1,0:T(8,128)(2,1)}, u32[]{:S(2)}, u32[]{:S(2)}) %collective-permute-start.1) | collective-permute-done | bytes 262176 | tf_op jit(solution)/shard_map/while/body/eval_jaxpr/cond/branch_1_fun/ppermute | solution.py:284
  348.0 57.1 %conditional.4 = (bf16[64,2048]{1,0:T(8,128)(2,1)S(1)}) conditional(s32[]{:T(128)} %convert_element_type.46, bf16[64,2048]{1,0:T(8,128)(2,1)} %get-tuple-element.594, (s32[1,4,32,8]{3,2,1,0:T(8,128)S(1)}, s32[4]{0:T(128)S(1)}, bf16[4,32,2048]{2,1,0:T(8,128)(2,1)}, bf16[4,32,2048]{2,1,0:T(8,128)(2,1)S(1)}, bf16[64,2048]{1,0:T(8,128)(2,1)}, ...), branch_computations={%region_1.1_spmd, %region_2.2_spmd} | conditional | bytes 6291464 | solution.py:280
  348.0 2.5 dispatch.1
  350.5 21.7 %all_to_all.16 = bf16[16,16,3072]{2,1,0:T(8,128)(2,1)S(1)} all-to-all(bf16[16,16,3072]{2,1,0:T(8,128)(2,1)S(1)} %bitcast.32), channel_id=1, replica_groups=mesh['pipe'=4,'exp'=16,'pair'=2] {'exp'}, dimensions={0} | all-to-all | bytes 3145728 | tf_op jit(solution)/shard_map/while/body/eval_jaxpr/cond/branch_1_fun/all_to_all | solution.py:253
  372.2 9.9 %experts.1 = bf16[256,3072]{1,0:T(8,128)(2,1)S(1)} custom-call(bf16[256,3072]{1,0:T(8,128)(2,1)S(1)} %bitcast.30, bf16[2,2048,768]{2,1,0:T(8,128)(2,1)} %bitcast.33, bf16[2,2048,768]{2,1,0:T(8,128)(2,1)} %bitcast.34, bf16[2,768,2048]{2,1,0:T(8,128)(2,1)} %bitcast.35), custom_call_target="tpu_custom_call" | custom-call | tf_op jit(solution)/shard_map/while/body/eval_jaxpr/cond/branch_1_fun/experts/pallas_call | solution.py:275
  382.2 21.4 %all_to_all.17 = bf16[16,16,3072]{2,1,0:T(8,128)(2,1)S(1)} all-to-all(bf16[16,16,3072]{2,1,0:T(8,128)(2,1)S(1)} %bitcast.31), channel_id=1, replica_groups=mesh['pipe'=4,'exp'=16,'pair'=2] {'exp'}, dimensions={0} | all-to-all | bytes 3145728 | tf_op jit(solution)/shard_map/while/body/eval_jaxpr/cond/branch_1_fun/all_to_all | solution.py:253
  403.6 1.6 combine.1
  405.2 15.5 %conditional.5 = ((bf16[64,2048]{1,0:T(8,128)(2,1)}, bf16[64,2048]{1,0:T(8,128)(2,1)})) conditional(s32[]{:T(128)} %convert_element_type.45, (bf16[64,2048]{1,0:T(8,128)(2,1)}, bf16[64,2048]{1,0:T(8,128)(2,1)}) %tuple.53, bf16[64,2048]{1,0:T(8,128)(2,1)S(1)} %get-tuple-element.637), branch_computations={%region_3.3_spmd, %region_4.4_spmd} | conditional | bytes 2097256 | solution.py:286
  407.8 6.2 %collective-permute-done = bf16[64,2048]{1,0:T(8,128)(2,1)} collective-permute-done((bf16[64,2048]{1,0:T(8,128)(2,1)S(1)}, bf16[64,2048]{1,0:T(8,128)(2,1)}, u32[]{:S(2)}, u32[]{:S(2)}) %collective-permute-start) | collective-permute-done | bytes 262176 | tf_op jit(solution)/shard_map/while/body/eval_jaxpr/cond/branch_1_fun/ppermute | solution.py:284
  414.0 6.7 %collective-permute-done.1 = bf16[64,2048]{1,0:T(8,128)(2,1)} collective-permute-done((bf16[64,2048]{1,0:T(8,128)(2,1)S(1)}, bf16[64,2048]{1,0:T(8,128)(2,1)}, u32[]{:S(2)}, u32[]{:S(2)}) %collective-permute-start.1) | collective-permute-done | bytes 262176 | tf_op jit(solution)/shard_map/while/body/eval_jaxpr/cond/branch_1_fun/ppermute | solution.py:284
  420.7 49.1 %conditional.4 = (bf16[64,2048]{1,0:T(8,128)(2,1)S(1)}) conditional(s32[]{:T(128)} %convert_element_type.46, bf16[64,2048]{1,0:T(8,128)(2,1)} %get-tuple-element.594, (s32[1,4,32,8]{3,2,1,0:T(8,128)S(1)}, s32[4]{0:T(128)S(1)}, bf16[4,32,2048]{2,1,0:T(8,128)(2,1)}, bf16[4,32,2048]{2,1,0:T(8,128)(2,1)S(1)}, bf16[64,2048]{1,0:T(8,128)(2,1)}, ...), branch_computations={%region_1.1_spmd, %region_2.2_spmd} | conditional | bytes 6291464 | solution.py:280
  420.7 2.5 dispatch.1
  423.2 17.5 %all_to_all.16 = bf16[16,16,3072]{2,1,0:T(8,128)(2,1)S(1)} all-to-all(bf16[16,16,3072]{2,1,0:T(8,128)(2,1)S(1)} %bitcast.32), channel_id=1, replica_groups=mesh['pipe'=4,'exp'=16,'pair'=2] {'exp'}, dimensions={0} | all-to-all | bytes 3145728 | tf_op jit(solution)/shard_map/while/body/eval_jaxpr/cond/branch_1_fun/all_to_all | solution.py:253
  440.7 9.9 %experts.1 = bf16[256,3072]{1,0:T(8,128)(2,1)S(1)} custom-call(bf16[256,3072]{1,0:T(8,128)(2,1)S(1)} %bitcast.30, bf16[2,2048,768]{2,1,0:T(8,128)(2,1)} %bitcast.33, bf16[2,2048,768]{2,1,0:T(8,128)(2,1)} %bitcast.34, bf16[2,768,2048]{2,1,0:T(8,128)(2,1)} %bitcast.35), custom_call_target="tpu_custom_call" | custom-call | tf_op jit(solution)/shard_map/while/body/eval_jaxpr/cond/branch_1_fun/experts/pallas_call | solution.py:275
  450.7 17.5 %all_to_all.17 = bf16[16,16,3072]{2,1,0:T(8,128)(2,1)S(1)} all-to-all(bf16[16,16,3072]{2,1,0:T(8,128)(2,1)S(1)} %bitcast.31), channel_id=1, replica_groups=mesh['pipe'=4,'exp'=16,'pair'=2] {'exp'}, dimensions={0} | all-to-all | bytes 3145728 | tf_op jit(solution)/shard_map/while/body/eval_jaxpr/cond/branch_1_fun/all_to_all | solution.py:253
  468.2 1.6 combine.1
  470.0 8.0 %collective-permute-done.5 = bf16[4,32,2048]{2,1,0:T(8,128)(2,1)S(1)} collective-permute-done((bf16[4,32,2048]{2,1,0:T(8,128)(2,1)S(1)}, bf16[4,32,2048]{2,1,0:T(8,128)(2,1)S(1)}, u32[]{:S(2)}, u32[]{:S(2)}) %collective-permute-start.5) | collective-permute-done | bytes 524320 | tf_op jit(solution)/shard_map/ppermute | solution.py:294
  (43 shorter events, 25.2 us)
Async XLA Ops:
  0.0 6.5 %collective-permute-start.2 = (bf16[4,32,2048]{2,1,0:T(8,128)(2,1)}, bf16[4,32,2048]{2,1,0:T(8,128)(2,1)S(1)}, u32[]{:S(2)}, u32[]{:S(2)}) collective-permute-start(bf16[4,32,2048]{2,1,0:T(8,128)(2,1)} %param.13), channel_id=1, source_target_pairs={{0,1},{1,0},{2,3},{3,2},{4,5},{5,4},{6,7},{7,6},{8,9},{9,8},{10,11... | collective-permute-start | bytes 1572872 | tf_op jit(solution)/shard_map/ppermute | solution.py:257
  1.5 3.2 collective-permute-start.3
  3.3 3.2 collective-permute-start.4
  9.0 5.2 %collective-permute-start = (bf16[64,2048]{1,0:T(8,128)(2,1)S(1)}, bf16[64,2048]{1,0:T(8,128)(2,1)}, u32[]{:S(2)}, u32[]{:S(2)}) collective-permute-start(bf16[64,2048]{1,0:T(8,128)(2,1)S(1)} %param.3), channel_id=1, source_target_pairs={{0,32},{1,33},{32,64},{33,65},{64,96},{65,97},{2,34},{3,35},{34,66... | collective-permute-start | bytes 786440 | tf_op jit(solution)/shard_map/while/body/eval_jaxpr/cond/branch_1_fun/ppermute | solution.py:284
  10.3 9.4 %collective-permute-start.1 = (bf16[64,2048]{1,0:T(8,128)(2,1)S(1)}, bf16[64,2048]{1,0:T(8,128)(2,1)}, u32[]{:S(2)}, u32[]{:S(2)}) collective-permute-start(bf16[64,2048]{1,0:T(8,128)(2,1)S(1)} %param.3), channel_id=1, source_target_pairs={{0,33},{1,32},{32,65},{33,64},{64,97},{65,96},{2,35},{3,34},{34,67... | collective-permute-start | bytes 786440 | tf_op jit(solution)/shard_map/while/body/eval_jaxpr/cond/branch_1_fun/ppermute | solution.py:284
  20.8 6.5 %collective-permute-start = (bf16[64,2048]{1,0:T(8,128)(2,1)S(1)}, bf16[64,2048]{1,0:T(8,128)(2,1)}, u32[]{:S(2)}, u32[]{:S(2)}) collective-permute-start(bf16[64,2048]{1,0:T(8,128)(2,1)S(1)} %param.3), channel_id=1, source_target_pairs={{0,32},{1,33},{32,64},{33,65},{64,96},{65,97},{2,34},{3,35},{34,66... | collective-permute-start | bytes 786440 | tf_op jit(solution)/shard_map/while/body/eval_jaxpr/cond/branch_1_fun/ppermute | solution.py:284
  22.1 10.5 %collective-permute-start.1 = (bf16[64,2048]{1,0:T(8,128)(2,1)S(1)}, bf16[64,2048]{1,0:T(8,128)(2,1)}, u32[]{:S(2)}, u32[]{:S(2)}) collective-permute-start(bf16[64,2048]{1,0:T(8,128)(2,1)S(1)} %param.3), channel_id=1, source_target_pairs={{0,33},{1,32},{32,65},{33,64},{64,97},{65,96},{2,35},{3,34},{34,67... | collective-permute-start | bytes 786440 | tf_op jit(solution)/shard_map/while/body/eval_jaxpr/cond/branch_1_fun/ppermute | solution.py:284
  33.7 170.2 %collective-permute-start = (bf16[64,2048]{1,0:T(8,128)(2,1)S(1)}, bf16[64,2048]{1,0:T(8,128)(2,1)}, u32[]{:S(2)}, u32[]{:S(2)}) collective-permute-start(bf16[64,2048]{1,0:T(8,128)(2,1)S(1)} %param.3), channel_id=1, source_target_pairs={{0,32},{1,33},{32,64},{33,65},{64,96},{65,97},{2,34},{3,35},{34,66... | collective-permute-start | bytes 786440 | tf_op jit(solution)/shard_map/while/body/eval_jaxpr/cond/branch_1_fun/ppermute | solution.py:284
  35.0 174.8 %collective-permute-start.1 = (bf16[64,2048]{1,0:T(8,128)(2,1)S(1)}, bf16[64,2048]{1,0:T(8,128)(2,1)}, u32[]{:S(2)}, u32[]{:S(2)}) collective-permute-start(bf16[64,2048]{1,0:T(8,128)(2,1)S(1)} %param.3), channel_id=1, source_target_pairs={{0,33},{1,32},{32,65},{33,64},{64,97},{65,96},{2,35},{3,34},{34,67... | collective-permute-start | bytes 786440 | tf_op jit(solution)/shard_map/while/body/eval_jaxpr/cond/branch_1_fun/ppermute | solution.py:284
  259.4 13.3 %collective-permute-start = (bf16[64,2048]{1,0:T(8,128)(2,1)S(1)}, bf16[64,2048]{1,0:T(8,128)(2,1)}, u32[]{:S(2)}, u32[]{:S(2)}) collective-permute-start(bf16[64,2048]{1,0:T(8,128)(2,1)S(1)} %param.3), channel_id=1, source_target_pairs={{0,32},{1,33},{32,64},{33,65},{64,96},{65,97},{2,34},{3,35},{34,66... | collective-permute-start | bytes 786440 | tf_op jit(solution)/shard_map/while/body/eval_jaxpr/cond/branch_1_fun/ppermute | solution.py:284
  260.7 18.5 %collective-permute-start.1 = (bf16[64,2048]{1,0:T(8,128)(2,1)S(1)}, bf16[64,2048]{1,0:T(8,128)(2,1)}, u32[]{:S(2)}, u32[]{:S(2)}) collective-permute-start(bf16[64,2048]{1,0:T(8,128)(2,1)S(1)} %param.3), channel_id=1, source_target_pairs={{0,33},{1,32},{32,65},{33,64},{64,97},{65,96},{2,35},{3,34},{34,67... | collective-permute-start | bytes 786440 | tf_op jit(solution)/shard_map/while/body/eval_jaxpr/cond/branch_1_fun/ppermute | solution.py:284
  328.8 13.7 %collective-permute-start = (bf16[64,2048]{1,0:T(8,128)(2,1)S(1)}, bf16[64,2048]{1,0:T(8,128)(2,1)}, u32[]{:S(2)}, u32[]{:S(2)}) collective-permute-start(bf16[64,2048]{1,0:T(8,128)(2,1)S(1)} %param.3), channel_id=1, source_target_pairs={{0,32},{1,33},{32,64},{33,65},{64,96},{65,97},{2,34},{3,35},{34,66... | collective-permute-start | bytes 786440 | tf_op jit(solution)/shard_map/while/body/eval_jaxpr/cond/branch_1_fun/ppermute | solution.py:284
  330.1 17.9 %collective-permute-start.1 = (bf16[64,2048]{1,0:T(8,128)(2,1)S(1)}, bf16[64,2048]{1,0:T(8,128)(2,1)}, u32[]{:S(2)}, u32[]{:S(2)}) collective-permute-start(bf16[64,2048]{1,0:T(8,128)(2,1)S(1)} %param.3), channel_id=1, source_target_pairs={{0,33},{1,32},{32,65},{33,64},{64,97},{65,96},{2,35},{3,34},{34,67... | collective-permute-start | bytes 786440 | tf_op jit(solution)/shard_map/while/body/eval_jaxpr/cond/branch_1_fun/ppermute | solution.py:284
  405.2 8.8 %collective-permute-start = (bf16[64,2048]{1,0:T(8,128)(2,1)S(1)}, bf16[64,2048]{1,0:T(8,128)(2,1)}, u32[]{:S(2)}, u32[]{:S(2)}) collective-permute-start(bf16[64,2048]{1,0:T(8,128)(2,1)S(1)} %param.3), channel_id=1, source_target_pairs={{0,32},{1,33},{32,64},{33,65},{64,96},{65,97},{2,34},{3,35},{34,66... | collective-permute-start | bytes 786440 | tf_op jit(solution)/shard_map/while/body/eval_jaxpr/cond/branch_1_fun/ppermute | solution.py:284
  406.5 14.1 %collective-permute-start.1 = (bf16[64,2048]{1,0:T(8,128)(2,1)S(1)}, bf16[64,2048]{1,0:T(8,128)(2,1)}, u32[]{:S(2)}, u32[]{:S(2)}) collective-permute-start(bf16[64,2048]{1,0:T(8,128)(2,1)S(1)} %param.3), channel_id=1, source_target_pairs={{0,33},{1,32},{32,65},{33,64},{64,97},{65,96},{2,35},{3,34},{34,67... | collective-permute-start | bytes 786440 | tf_op jit(solution)/shard_map/while/body/eval_jaxpr/cond/branch_1_fun/ppermute | solution.py:284
  469.9 8.1 %collective-permute-start.5 = (bf16[4,32,2048]{2,1,0:T(8,128)(2,1)S(1)}, bf16[4,32,2048]{2,1,0:T(8,128)(2,1)S(1)}, u32[]{:S(2)}, u32[]{:S(2)}) collective-permute-start(bf16[4,32,2048]{2,1,0:T(8,128)(2,1)S(1)} %constant_dynamic-slice_fusion), channel_id=1, source_target_pairs={{0,1},{1,0},{2,3},{3,2},{4,5},{5,4},{6,7},{7,6},{8,9},{9,8},{10,11... | collective-permute-start | bytes 1572872 | tf_op jit(solution)/shard_map/ppermute | solution.py:294
